TPU v7x, 32 devices: a whole 2x2x4 slice. The times are simulated.
32 devices in a mesh: gx: 4 (over y, x), gy: 2 (over core), gz: 4 (over z).
Axes of the slice: x: 2, y: 2, z: 4, core: 2. Of those that a mesh axis runs over, the one named last changes fastest.
Arguments:
- populations: float32 [2, 19, 16, 32, 512], P(None, None, 'gx', 'gy', 'gz'), may hold values from 0.01 to 0.2
- solid: int32 [16, 32, 512], P('gx', 'gy', 'gz'), may hold values 0 or 1
Outputs:
- read: float32 [2, 19, 16, 32, 512], P(None, None, 'gx', 'gy', 'gz')
All inputs are finite; a program needn't handle non-finite values. No bound on the sum of `solid` on one device may be relied on, other than what follows from the above.
Results may differ from a plain program's by a relative error of at most 0.0001.
Values sent between devices are 32-bit elements; how exact they have to be, the bound alone decides.
A program may use at most 64 MiB of HBM per device.

v0:
```python
import jax
import jax.numpy as jnp
from jax import lax
from jax.experimental import pallas as pl
from jax.experimental.pallas import tpu as pltpu
from jax.sharding import PartitionSpec as P

VELOCITIES = [
    (0, 0, 0),
    (1, 0, 0),
    (-1, 0, 0),
    (0, 1, 0),
    (0, -1, 0),
    (0, 0, 1),
    (0, 0, -1),
    (1, 1, 0),
    (-1, -1, 0),
    (1, -1, 0),
    (-1, 1, 0),
    (1, 0, 1),
    (-1, 0, -1),
    (1, 0, -1),
    (-1, 0, 1),
    (0, 1, 1),
    (0, -1, -1),
    (0, 1, -1),
    (0, -1, 1),
]
WEIGHTS = [1.0 / 3.0] + [1.0 / 18.0] * 6 + [1.0 / 36.0] * 12
OPPOSITE = [0, 2, 1, 4, 3, 6, 5, 8, 7, 10, 9, 12, 11, 14, 13, 16, 15, 18, 17]
COUPLING = 0.9
RELAX = (1.0, 0.8)
WALL = (0.3, 1.5)
AXES = ("gx", "gy", "gz")
MESH = pl.DeviceIdType.MESH

ORDER = (
    [0]
    + [i for i in range(19) if VELOCITIES[i][0] == 1]
    + [i for i in range(19) if VELOCITIES[i][0] == -1]
    + [i for i in range(1, 19) if VELOCITIES[i][0] == 0]
)
SLOT = {i: s for s, i in enumerate(ORDER)}
Z_UP = [i for i in range(19) if VELOCITIES[i][2] == 1]
Z_PAIR = {}
for _g, _i in enumerate(Z_UP):
    Z_PAIR[_i] = _g
    Z_PAIR[OPPOSITE[_i]] = _g
Z_OFFSETS = [v for v in VELOCITIES if v[2] != 0]
Z_INDEX = {v: n for n, v in enumerate(Z_OFFSETS)}
T = 8
LANES = 128


def step_kernel(pop_hbm, solid_hbm, out, pop, solid, psi, zpsi, post, zpost, vel, source,
                pack1, recv1, pack2, recv2, face, ghost, load_sem, send1, got1, send2, got2):
    X, Y, Z = solid.shape
    YT = Y // T
    lo, hi = slice(T, 2 * T), slice(Y, Y + T)
    low_halo, high_halo = slice(0, T), slice(Y + T, Y + 2 * T)
    inner = slice(T, Y + T)

    loads = [pltpu.make_async_copy(solid_hbm, solid, load_sem.at[X])]
    loads += [
        pltpu.make_async_copy(pop_hbm.at[:, :, x], pop.at[:, :, x], load_sem.at[x])
        for x in range(X)
    ]

    me = [lax.axis_index(a) for a in AXES]
    count = [lax.axis_size(a) for a in AXES]

    def device(offset):
        return tuple(lax.rem(me[d] + offset[d] + count[d], count[d]) for d in range(3))

    barrier = pltpu.get_barrier_semaphore()
    greeted = sorted(VELOCITIES[1:], key=lambda v: (-abs(v[2]), -abs(v[0]), -abs(v[1])))
    for offset in greeted:
        pl.semaphore_signal(barrier, inc=1, device_id=device(offset), device_id_type=MESH)
    for copy in loads:
        copy.start()

    lane = lax.broadcasted_iota(jnp.int32, (T, LANES), 1)
    pair = lane // 2
    lane_y = lax.broadcasted_iota(jnp.int32, (Y, LANES), 1)
    first, last = lane_y == 0, lane_y == Z - 1

    loads[0].wait()
    inv = [1.0 / t for t in RELAX]
    packed = jnp.zeros((T, LANES), jnp.float32)

    def combo1(k, x, t):
        return (k * X + x) * YT + t

    for x in range(X):
        loads[1 + x].wait()
        fluid = solid[x] == 0
        total, mom = [], [[], [], []]
        for k in range(2):
            f = [pop[k, i, x] for i in range(19)]
            rho = f[0]
            m = [None, None, None]
            for i in range(1, 19, 2):
                rho = rho + (f[i] + f[i + 1])
                diff = f[i] - f[i + 1]
                for d in range(3):
                    c = VELOCITIES[i][d]
                    if c:
                        m[d] = (
                            (diff if c > 0 else -diff)
                            if m[d] is None
                            else (m[d] + diff if c > 0 else m[d] - diff)
                        )
            total.append(rho)
            signed = jnp.where(fluid, rho, -WALL[k])
            psi[k, 1 + x, inner] = signed
            for d in range(3):
                mom[d].append(m[d] * inv[k] if inv[k] != 1.0 else m[d])
            for t in range(YT):
                j = combo1(k, x, t)
                piece = pltpu.roll(signed[t * T:(t + 1) * T], (2 * j + 1) % LANES, 1)
                packed = jnp.where(pair == j, piece, packed)
        scale = 1.0 / (total[0] * inv[0] + total[1] * inv[1])
        for d in range(3):
            vel[d, x] = (mom[d][0] + mom[d][1]) * scale
    pack1[...] = packed

    pl.semaphore_wait(barrier, len(greeted))

    def remote(src, dst, send, recv, n, offset):
        return pltpu.make_async_remote_copy(
            src_ref=src,
            dst_ref=dst,
            send_sem=send.at[n],
            recv_sem=recv.at[n],
            device_id=device(offset),
            device_id_type=MESH,
        )

    def edge_of(offset):
        dx, dy, _ = offset
        src_x = slice(1, X + 1) if dx == 0 else (slice(X, X + 1) if dx > 0 else slice(1, 2))
        dst_x = slice(1, X + 1) if dx == 0 else (slice(0, 1) if dx > 0 else slice(X + 1, X + 2))
        src_y = inner if dy == 0 else (hi if dy > 0 else lo)
        dst_y = inner if dy == 0 else (low_halo if dy > 0 else high_halo)
        return (src_x, src_y), (dst_x, dst_y)

    order = sorted(range(1, 19), key=lambda i: -sum(abs(c) for c in VELOCITIES[i][::2]))
    copies1 = {}
    for offset in sorted(greeted, key=lambda v: (-abs(v[2]), -abs(v[0]), -abs(v[1]))):
        n = len(copies1)
        if offset[2]:
            copy = remote(pack1, recv1.at[Z_INDEX[offset]], send1, got1, n, offset)
        else:
            s, d = edge_of(offset)
            copy = remote(psi.at[:, s[0], s[1]], psi.at[:, d[0], d[1]], send1, got1, n, offset)
        copy.start()
        copies1[offset] = copy
    raw = []
    for side in (1, -1):
        for i in range(19):
            if VELOCITIES[i][0] == side:
                src_plane, dst_plane = (X - 1, 0) if side > 0 else (0, X + 1)
                copy = remote(pop.at[1, i, src_plane], post.at[1, SLOT[i], dst_plane, inner],
                              send1, got1, 18 + len(raw), (side, 0, 0))
                copy.start()
                raw.append(copy)
    for dz in (1, -1):
        copies1[(0, 0, dz)].wait_recv()
    for offset in greeted:
        if offset[:2] != (0, 0) and not (offset[0] and offset[2]):
            copies1[offset].wait_recv()

    def came1(x, y, z):
        return recv1[Z_INDEX[(-x, -y, -z)]]

    def put1(merged, k, x, t, plane, rows):
        zpsi[k, plane, rows] = pltpu.roll(merged, (LANES - 2 * combo1(k, x, t) - 1) % LANES, 1)

    even = lane % 2 == 0

    def unpack1(dx, dy):
        merged = jnp.where(even, came1(dx, dy, -1), came1(dx, dy, 1))
        xs = range(X) if dx == 0 else ([X - 1] if dx < 0 else [0])
        ts = range(YT) if dy == 0 else ([YT - 1] if dy < 0 else [0])
        for k in range(2):
            for x in xs:
                for t in ts:
                    plane = 1 + x + dx * X
                    row = T * (1 + t + dy * YT)
                    put1(merged, k, x, t, plane, slice(row, row + T))

    for dx, dy in ((0, 0), (0, -1), (0, 1)):
        unpack1(dx, dy)

    def shifted(base, edge, move):
        if move[2] == 0:
            return base
        if move[2] > 0:
            return pltpu.roll(jnp.where(first, edge, base), Z - 1, 1)
        return pltpu.roll(jnp.where(last, edge, base), 1, 1)

    half = X // 2

    def combo2(k, g, x, t):
        return (((x % half) * 2 + k) * 5 + g) * YT + t

    def equilibrium(pairs, rho_of, u):
        flat = 1.0 - 1.5 * (u[0] * u[0] + u[1] * u[1] + u[2] * u[2])
        result = {}
        for i, signs in pairs:
            if i == 0:
                result[0] = rho_of[WEIGHTS[0]] * flat
                continue
            along = None
            for d in range(3):
                c = VELOCITIES[i][d]
                if c:
                    along = (
                        (u[d] if c > 0 else -u[d])
                        if along is None
                        else (along + u[d] if c > 0 else along - u[d])
                    )
            w = rho_of[WEIGHTS[i]]
            even_part = w * (flat + 4.5 * (along * along))
            odd_part = w * (3.0 * along)
            if 1 in signs:
                result[i] = even_part + odd_part
            if -1 in signs:
                result[i + 1] = even_part - odd_part
        return result

    everything = [(0, (1,))] + [(i, (1, -1)) for i in range(1, 19, 2)]
    copies2 = []
    kinds = []

    def launch2(src, dst, offset):
        copy = remote(src, dst, send2, got2, len(copies2), offset)
        copy.start()
        copies2.append(copy)
        kinds.append(tuple(abs(c) for c in offset))

    packs = [jnp.zeros((T, LANES), jnp.float32) for _ in range(2)]
    for x in list(range(1, X - 1)) + [0, X - 1]:
        if x == 0:
            for dx in (1, -1):
                for dz in (1, -1):
                    copies1[(dx, 0, dz)].wait_recv()
            for dx in (1, -1):
                unpack1(dx, 0)
        grads = []
        for k in range(2):
            parts = [None, None, None]
            beside = {}
            for i in range(1, 19):
                c = VELOCITIES[i]
                at = (k, 1 + x + c[0], slice(T + c[1], T + c[1] + Y))
                value = shifted(psi[at], zpsi[at] if c[2] else None, c)
                if k == 0:
                    source[OPPOSITE[i], x] = value
                beside[i] = jnp.abs(value)
            for i in range(1, 19, 2):
                term = WEIGHTS[i] * (beside[i] - beside[i + 1])
                for d in range(3):
                    c = VELOCITIES[i][d]
                    if c:
                        parts[d] = (
                            (term if c > 0 else -term)
                            if parts[d] is None
                            else (parts[d] + term if c > 0 else parts[d] - term)
                        )
            grads.append(parts)
        for k in range(2):
            u = [vel[d, x] - (COUPLING * RELAX[k]) * grads[1 - k][d] for d in range(3)]
            rho = jnp.abs(psi[k, 1 + x, inner]) * inv[k]
            keep = 1.0 - inv[k]
            values = equilibrium(everything, {w: rho * w for w in sorted(set(WEIGHTS))}, u)
            for i in range(19):
                if abs(keep) > 1e-9:
                    values[i] = values[i] + keep * pop[k, i, x]
                post[k, SLOT[i], 1 + x, inner] = values[i]
            if x in (0, X - 1):
                for d in range(3):
                    face[int(x != 0), 3 * k + d] = u[d]
            for g, i in enumerate(Z_UP):
                ends = jnp.where(last, values[i], values[OPPOSITE[i]])
                for t in range(YT):
                    j = combo2(k, g, x, t)
                    piece = pltpu.roll(ends[t * T:(t + 1) * T], (2 * j + 1) % LANES, 1)
                    packs[x // half] = jnp.where(pair == j, piece, packs[x // half])
        if x in (0, X - 1):
            side = int(x != 0)
            launch2(face.at[side], ghost.at[1 - side], (2 * side - 1, 0, 0))
    for h in range(2):
        pack2[h] = packs[h]

    for i in order:
        offset = VELOCITIES[i]
        if offset[2]:
            halves = slice(0, 2) if offset[0] == 0 else (slice(1, 2) if offset[0] > 0 else slice(0, 1))
            launch2(pack2.at[halves], recv2.at[Z_INDEX[offset], halves], offset)
            continue
        s, d = edge_of(offset)
        if offset[0] and offset[1]:
            launch2(post.at[:, SLOT[i], s[0], s[1]], post.at[:, SLOT[i], d[0], d[1]], offset)
        elif offset[1]:
            for q in range(19):
                if VELOCITIES[q][1] == offset[1]:
                    launch2(post.at[:, SLOT[q], s[0], s[1]], post.at[:, SLOT[q], d[0], d[1]], offset)

    def await2(*wanted):
        for copy, kind in zip(copies2, kinds):
            if kind in wanted:
                copy.wait_recv()

    def stream(x, still_z):
        fluid = solid[x] == 0
        for k in range(2):
            for i in range(19):
                c = VELOCITIES[i]
                if (c[2] == 0) != still_z:
                    continue
                rows = slice(T - c[1], T - c[1] + Y)
                read = post[k, SLOT[i], 1 + x - c[0], rows]
                if i:
                    edge = zpost[k, Z_PAIR[i], 1 + x - c[0], rows] if c[2] else None
                    read = shifted(read, edge, tuple(-a for a in c))
                    bounced = post[k, SLOT[OPPOSITE[i]], 1 + x, inner]
                    read = jnp.where(source[i, x] > 0.0, read, bounced)
                out[k, i, x] = jnp.where(fluid, read, pop[k, i, x])

    await2((0, 1, 0))
    for x in range(1, X - 1):
        stream(x, True)

    for copy in raw:
        copy.wait_recv()
    await2((1, 0, 0))
    for side in range(2):
        plane = 0 if side == 0 else X + 1
        sign = 1 if side == 0 else -1
        wanted = []
        for i in range(1, 19, 2):
            if VELOCITIES[i][0]:
                wanted.append((i, (sign * VELOCITIES[i][0],)))
        for k in range(2):
            rho = jnp.abs(psi[k, plane, inner]) * inv[k]
            u = [ghost[side, 3 * k + d] for d in range(3)]
            keep = 1.0 - inv[k]
            values = equilibrium(wanted, {w: rho * w for w in sorted(set(WEIGHTS))}, u)
            for i in values:
                value = values[i]
                if abs(keep) > 1e-9:
                    value = value + keep * post[k, SLOT[i], plane, inner]
                post[k, SLOT[i], plane, inner] = value
    await2((1, 1, 0))
    for x in (0, X - 1):
        stream(x, True)
    await2((0, 0, 1), (0, 1, 1))

    def came2(x, y, z, h):
        return recv2[Z_INDEX[(-x, -y, -z)], h]

    def put2(tile, k, g, x, t, plane, rows):
        zpost[k, g, plane, rows] = pltpu.roll(tile, (LANES - 2 * combo2(k, g, x, t) - 1) % LANES, 1)

    for h in range(2):
        merged = jnp.where(even, came2(0, 0, -1, h), came2(0, 0, 1, h))
        for x in range(h * half, (h + 1) * half):
            for k in range(2):
                for g in range(5):
                    for t in range(YT):
                        row = T * (1 + t)
                        put2(merged, k, g, x, t, 1 + x, slice(row, row + T))
    def edges2(along_x):
        for i in range(1, 19):
            c = VELOCITIES[i]
            if c[2] == 0 or not c[0 if along_x else 1]:
                continue
            g = Z_PAIR[i]
            for k in range(2):
                if c[0]:
                    x = X - 1 if c[0] > 0 else 0
                    plane = 0 if c[0] > 0 else X + 1
                    for t in range(YT):
                        row = T * (1 + t)
                        put2(came2(-c[0], 0, -c[2], x // half), k, g, x, t, plane, slice(row, row + T))
                else:
                    t = YT - 1 if c[1] > 0 else 0
                    rows = low_halo if c[1] > 0 else high_halo
                    for x in range(X):
                        put2(came2(0, -c[1], -c[2], x // half), k, g, x, t, 1 + x, rows)

    edges2(False)
    for x in range(1, X - 1):
        stream(x, False)
    await2((1, 0, 1))
    edges2(True)
    for x in (0, X - 1):
        stream(x, False)
    for copy in list(copies1.values()) + raw + copies2:
        copy.wait_send()


def body(populations, solid):
    X, Y, Z = solid.shape
    f32 = jnp.float32
    dma = pltpu.SemaphoreType.DMA
    return pl.pallas_call(
        step_kernel,
        out_shape=pltpu.VMEM(populations.shape, f32),
        in_specs=[pl.BlockSpec(memory_space=pl.ANY)] * 2,
        out_specs=pl.BlockSpec(memory_space=pltpu.VMEM),
        scratch_shapes=[
            pltpu.VMEM(populations.shape, f32),
            pltpu.VMEM(solid.shape, jnp.int32),
            pltpu.VMEM((2, X + 2, Y + 2 * T, Z), f32),
            pltpu.VMEM((2, X + 2, Y + 2 * T, Z), f32),
            pltpu.VMEM((2, 19, X + 2, Y + 2 * T, Z), f32),
            pltpu.VMEM((2, 5, X + 2, Y + 2 * T, Z), f32),
            pltpu.VMEM((3, X, Y, Z), f32),
            pltpu.VMEM((19, X, Y, Z), f32),
            pltpu.VMEM((T, LANES), f32),
            pltpu.VMEM((10, T, LANES), f32),
            pltpu.VMEM((2, T, LANES), f32),
            pltpu.VMEM((10, 2, T, LANES), f32),
            pltpu.VMEM((2, 6, Y, Z), f32),
            pltpu.VMEM((2, 6, Y, Z), f32),
            dma((X + 1,)),
            dma((28,)),
            dma((28,)),
            dma((26,)),
            dma((26,)),
        ],
        compiler_params=pltpu.CompilerParams(collective_id=0, has_side_effects=True),
    )(populations, solid)


def solution(mesh):
    in_specs = (P(None, None, "gx", "gy", "gz"), P("gx", "gy", "gz"))
    out_specs = P(None, None, "gx", "gy", "gz")
    return jax.shard_map(body, mesh=mesh, in_specs=in_specs, out_specs=out_specs, check_vma=False)
```

profile of v0, /device:TPU:0, one launch (start us, length us, event | category | flops | bytes accessed | tf_op | source)
XLA Modules:
  0.0 18.9 jit_solution(15606417137851025467)
XLA Ops:
  0.0 17.9 %shard_map.28 = f32[2,19,4,16,128]{4,3,2,1,0:T(8,128)S(1)} custom-call(f32[2,19,4,16,128]{4,3,2,1,0:T(8,128)} %pop_hbm.1, s32[4,16,128]{2,1,0:T(8,128)} %solid_hbm.1), custom_call_target="tpu_custom_call" | custom-call | tf_op jit(solution)/shard_map/pallas_call | solution.py:408
  17.9 1.0 %copy.4 = f32[2,19,4,16,128]{4,3,2,1,0:T(8,128)} copy(f32[2,19,4,16,128]{4,3,2,1,0:T(8,128)S(1)} %shard_map.28) | data formatting | bytes 2490368
where the time goes:
time: 19.1 us; the launch traced here: 18.9 us
  Pallas kernels  17.9 us (94%)
  local copies, waits for them, and re-layouts  1.04 us (5%)
    pallas_call x1, Pallas kernels, body(): pl.pallas_call(step_kernel, out_shape=pltpu.VMEM(populations.shape, f32),...  17.9 us
    unnamed x1, local copies, waits for them, and re-layouts  1.04 us

commit v1 on v0

v1 whole, which is shorter than its diff:
```python
import jax
import jax.numpy as jnp
from jax import lax
from jax.experimental import pallas as pl
from jax.experimental.pallas import tpu as pltpu
from jax.sharding import PartitionSpec as P

VELOCITIES = [
    (0, 0, 0),
    (1, 0, 0),
    (-1, 0, 0),
    (0, 1, 0),
    (0, -1, 0),
    (0, 0, 1),
    (0, 0, -1),
    (1, 1, 0),
    (-1, -1, 0),
    (1, -1, 0),
    (-1, 1, 0),
    (1, 0, 1),
    (-1, 0, -1),
    (1, 0, -1),
    (-1, 0, 1),
    (0, 1, 1),
    (0, -1, -1),
    (0, 1, -1),
    (0, -1, 1),
]
WEIGHTS = [1.0 / 3.0] + [1.0 / 18.0] * 6 + [1.0 / 36.0] * 12
OPPOSITE = [0, 2, 1, 4, 3, 6, 5, 8, 7, 10, 9, 12, 11, 14, 13, 16, 15, 18, 17]
INDEX = {v: i for i, v in enumerate(VELOCITIES)}
COUPLING = 0.9
RELAX = (1.0, 0.8)
WALL = (0.3, 1.5)
INV = [1.0 / t for t in RELAX]
KEEP = [1.0 - v for v in INV]
AXES = ("gx", "gy", "gz")
MESH = pl.DeviceIdType.MESH

X_UP = [i for i in range(19) if VELOCITIES[i][0] == 1]
Y_UP = [i for i in range(19) if VELOCITIES[i][1] == 1]
Z_UP = [(0, 0, 1), (1, 0, 1), (-1, 0, 1), (0, 1, 1), (0, -1, 1)]
Z_UP = [INDEX[v] for v in Z_UP]
Z_PAIR = {}
for _g, _i in enumerate(Z_UP):
    Z_PAIR[_i] = _g
    Z_PAIR[OPPOSITE[_i]] = _g
Z_FROM = [(dx, dz) for dz in (-1, 1) for dx in (0, -1, 1)]
T = 8
LANES = 128
HALF = LANES // 2


def along_of(i, u):
    total = None
    for d in range(3):
        c = VELOCITIES[i][d]
        if c:
            term = u[d] if c > 0 else -u[d]
            total = term if total is None else total + term
    return total


def step_kernel(pop_hbm, solid_hbm, out, pop, solid, S, SU, SD, psi, H, O, A, V, post, zpost,
                YS, YV, YP, WP, XP, XW, XWR, XPW, ZS, XA, ZR, load_sem, send_sem, recv_sem,
                near_sem, far_sem):
    X, Y, Z = solid.shape
    YT = Y // T
    inner = slice(T, T + Y)
    low, high = slice(0, T), slice(Y + T, Y + 2 * T)
    XX = X + 4
    assert Z == LANES and (YT + 2) * XX * 2 <= HALF and X >= 2
    stride_t = HALF // (YT + 2)
    assert stride_t >= 2 * XX and 2 * X <= XX

    loads = [pltpu.make_async_copy(solid_hbm, solid, load_sem.at[X])]
    loads += [
        pltpu.make_async_copy(pop_hbm.at[:, :, x], pop.at[:, :, x], load_sem.at[x])
        for x in range(X)
    ]

    me = [lax.axis_index(a) for a in AXES]
    count = [lax.axis_size(a) for a in AXES]
    assert count[1] % 2 == 0
    parity = lax.rem(me[1], 2)
    is_near, is_far = parity == 0, parity == 1

    def device(offset):
        return tuple(lax.rem(me[d] + offset[d] + count[d], count[d]) for d in range(3))

    def member(offset, odd):
        place = device(offset)
        return (place[0], me[1] - parity + odd, place[2])

    barrier = pltpu.get_barrier_semaphore()

    def arrive(place):
        pl.semaphore_signal(barrier, inc=1, device_id=place, device_id_type=MESH)

    for dx, dz in sorted(Z_FROM, key=lambda v: -abs(v[0])):
        arrive(member((dx, 0, dz), 1))
    for dx in (1, -1):
        arrive(member((dx, 0, 0), 0))
    arrive((me[0], me[1] + 1 - 2 * parity, me[2]))
    near_count, far_count = 5, 13
    if count[1] > 2:
        near_count += 2
        arrive((me[0], lax.rem(me[1] + 3 * parity - 2 + count[1], count[1]), me[2]))
    partner = (me[0], me[1] + 1 - 2 * parity, me[2])
    for copy in loads:
        copy.start()

    lane = lax.broadcasted_iota(jnp.int32, (T, LANES), 1)
    row = lax.broadcasted_iota(jnp.int32, (T, LANES), 0)
    pair = lane // 2
    even = lane % 2 == 0
    half = lane // HALF
    slot = (lane % stride_t) // 2
    tile_t = (lane % HALF) // stride_t
    first, last = lane == 0, lane == Z - 1
    lane_y = lax.broadcasted_iota(jnp.int32, (Y, LANES), 1)
    first_y, last_y = lane_y == 0, lane_y == Z - 1
    upper = row < T // 2

    def roll(v, n):
        n = n % LANES
        return pltpu.roll(v, n, 1) if n else v

    def roll_rows(v, n):
        n = n % T
        return pltpu.roll(v, n, 0) if n else v

    copies = {}

    def send(name, src, dst, offset):
        n = len(copies)
        copy = pltpu.make_async_remote_copy(
            src_ref=src,
            dst_ref=dst,
            send_sem=send_sem.at[n],
            recv_sem=recv_sem.at[n],
            device_id=device(offset),
            device_id_type=MESH,
        )
        copy.start()
        assert name not in copies
        copies[name] = copy

    def await_(kind):
        for name, copy in copies.items():
            if name[0] == kind:
                copy.wait_recv()

    loads[0].wait()
    for x in range(X):
        loads[1 + x].wait()
        fluid = solid[x] == 0
        total, mom = [], []
        for k in range(2):
            f = [pop[k, i, x] for i in range(19)]
            rho = f[0]
            m = [None, None, None]
            for i in range(1, 19, 2):
                rho = rho + (f[i] + f[i + 1])
                diff = f[i] - f[i + 1]
                for d in range(3):
                    c = VELOCITIES[i][d]
                    if c:
                        m[d] = (
                            (diff if c > 0 else -diff)
                            if m[d] is None
                            else (m[d] + diff if c > 0 else m[d] - diff)
                        )
            total.append(rho)
            S[k, 2 + x, inner] = jnp.where(fluid, rho, -WALL[k])
            mom.append([v * INV[k] if INV[k] != 1.0 else v for v in m])
        scale = 1.0 / (total[0] * INV[0] + total[1] * INV[1])
        for d in range(3):
            V[d, 1 + x, 0:Y] = (mom[0][d] + mom[1][d]) * scale

    @pl.when(is_near)
    def _():
        pl.semaphore_wait(barrier, near_count)
        pl.semaphore_signal(near_sem, inc=1, device_id=partner, device_id_type=MESH)

    @pl.when(is_far)
    def _():
        pl.semaphore_wait(near_sem, 1)

    for n, side in enumerate((1, -1)):
        tile = slice(Y - T, Y) if side > 0 else slice(0, T)
        wide = slice(Y, Y + T) if side > 0 else slice(T, 2 * T)
        to = (0, side, 0)
        send(("yS", side), S.at[:, 2:2 + X, wide], YS.at[n], to)
        send(("yV", side), V.at[:, 1:1 + X, tile], YV.at[n], to)
        for m, i in enumerate(Y_UP):
            i = i if side > 0 else OPPOSITE[i]
            send(("yP", side, m), pop.at[1, i, :, tile], YP.at[n, m], to)
    for n, side in enumerate((1, -1)):
        to = (side, 0, 0)
        src = slice(X, X + 2) if side > 0 else slice(2, 4)
        dst = slice(0, 2) if side > 0 else slice(X + 2, X + 4)
        send(("xS", side), S.at[:, src, inner], S.at[:, dst, inner], to)
    for n, side in enumerate((1, -1)):
        to = (side, 0, 0)
        src, dst = (X, 0) if side > 0 else (1, X + 1)
        send(("xV", side), V.at[:, src, 0:Y], V.at[:, dst, 0:Y], to)
    for m, i in enumerate(X_UP):
        for n, side in enumerate((1, -1)):
            i_s, x_s = (i, X - 1) if side > 0 else (OPPOSITE[i], 0)
            send(("xP", side, m), pop.at[1, i_s, x_s], XP.at[n, m], (side, 0, 0))

    def place_of(h, b, t, x):
        return (h * HALF + t * stride_t + (b * X + x) * 2) // 2

    blank = jnp.zeros((T, LANES), jnp.float32)
    packs = [blank, blank, blank, blank]

    def put(p, h, b, t, x, value):
        j = place_of(h, b, t, x)
        packs[p] = jnp.where(pair == j, roll(value, 2 * j + 1), packs[p])

    POP_PLACE = [(2, 0, 0), (2, 0, 1), (2, 1, 0), (2, 1, 1), (3, 1, 0)]
    V_PLACE = [(1, 0, 0), (1, 0, 1), (1, 1, 0)]

    def second(value):
        return jnp.where(lane < HALF, roll(value, -1), roll(value, 1))

    def pack(x, t):
        rows = low if t == 0 else slice(T * t, T * t + T)
        rows_v = slice(Y, Y + T) if t == 0 else slice(T * (t - 1), T * t)
        for k in range(2):
            value = S[k, 2 + x, rows]
            put(0, k, 0, t, x, value)
            put(0, k, 1, t, x, second(value))
        for d in range(3):
            put(*V_PLACE[d], t, x, V[d, 1 + x, rows_v])
        for g, i in enumerate(Z_UP):
            if t == 0:
                c = VELOCITIES[i]
                if c[1] == 0:
                    continue
                y_dir = i if c[1] > 0 else OPPOSITE[i]
                value = WP[Y_UP.index(y_dir), x]
            else:
                rows_p = slice(T * (t - 1), T * t)
                value = jnp.where(lane < HALF, pop[1, OPPOSITE[i], x, rows_p], pop[1, i, x, rows_p])
            put(*POP_PLACE[g], t, x, value)

    for x in range(X):
        for t in range(1, YT + 1):
            pack(x, t)

    await_("yS")
    await_("yV")
    await_("yP")
    for x in range(X):
        for k in range(2):
            value = jnp.where(upper, YS[1, k, x], YS[0, k, x])
            S[k, 2 + x, low] = value
            S[k, 2 + x, high] = value
        for d in range(3):
            V[d, 1 + x, Y:Y + T] = jnp.where(upper, YV[1, d, x], YV[0, d, x])
        for m in range(5):
            WP[m, x] = jnp.where(upper, YP[1, m, x], YP[0, m, x])
    for x in range(X):
        pack(x, 0)
    diag = jnp.where(((slot % X) == X - 1) == even, roll(packs[2], HALF), roll(packs[2], 2 * X))
    packs[1] = jnp.where((half == 1) & (slot >= X) & (slot < 2 * X), diag, packs[1])
    for p in range(4):
        ZS[p] = jnp.where(tile_t == YT + 1, roll(packs[p], stride_t * (YT + 1)), packs[p])

    pairs_y = [Y_UP.index(INDEX[(1, 1, 0)]), Y_UP.index(INDEX[(-1, 1, 0)])]
    keep_rows = (row < 2) | (row >= T - 2)
    for n, side in enumerate((1, -1)):
        planes = (X, X + 1) if side > 0 else (2, 3)
        for m, p in enumerate(planes):
            XW[n, m] = jnp.where(keep_rows, S[0, p, low], roll_rows(S[1, p, low], 4))
        x = X - 1 if side > 0 else 0
        up, down = (pairs_y[0], pairs_y[1]) if side > 0 else (pairs_y[1], pairs_y[0])
        fields = [V[d, 1 + x, Y:Y + T] for d in range(3)]
        fields.append(jnp.where(upper, WP[down, x], WP[up, x]))
        merged = fields[0]
        for f in range(1, 4):
            at = (row == 2 * f - 1) | (row == 2 * f)
            merged = jnp.where(at, roll_rows(fields[f], 2 * f), merged)
        XW[n, 2] = merged
    for n, side in enumerate((1, -1)):
        send(("xA", side), ZS.at[0], XA.at[n], (side, 0, 0))
        send(("xW", side), XW.at[n], XWR.at[n], (side, 0, 0))

    @pl.when(is_far)
    def _():
        pl.semaphore_wait(barrier, far_count)
        pl.semaphore_signal(far_sem, inc=1, device_id=partner, device_id_type=MESH)

    @pl.when(is_near)
    def _():
        pl.semaphore_wait(far_sem, 1)

    for dx, dz in sorted(Z_FROM, key=lambda v: -abs(v[0])):
        size = slice(0, 2) if dx else slice(0, 4)
        send(("z", dx, dz), ZS.at[size], ZR.at[Z_FROM.index((-dx, -dz)), size], (dx, 0, dz))

    await_("xS")
    await_("xA")
    await_("xW")
    for n in range(2):
        planes = (0, 1) if n == 0 else (X + 2, X + 3)
        for m, p in enumerate(planes):
            value = XWR[n, m]
            other = roll_rows(value, 4)
            for k, w in ((0, value), (1, other)):
                S[k, p, low] = w
                S[k, p, high] = w
    await_("z")

    def gather(b, middle, left, right):
        center = roll(middle, 2 * (2 - b * X))
        before = roll(left, -2 * (b * X + X - 2))
        after = roll(right, 2 * (X + 2 - b * X))
        return jnp.where(slot < 2, before, jnp.where(slot >= X + 2, after, center))

    def merged_z(dx, p):
        return jnp.where(even, ZR[Z_FROM.index((dx, -1)), p], ZR[Z_FROM.index((dx, 1)), p])

    def gather_z(p):
        m = [merged_z(dx, p) for dx in (0, -1, 1)]
        return gather(0, *m), gather(1, *m)

    s1, s2 = gather_z(0)
    s0 = gather(0, ZS[0], XA[0], XA[1])
    s0 = jnp.where(even, roll(s0, -1), roll(s0, 1))

    def spread(tile, k, t, xx):
        return roll(tile, LANES - 1 - (k * HALF + t * stride_t + 2 * xx))

    for p in range(XX):
        for k in range(2):
            for t in range(YT + 1):
                rows = low if t == 0 else slice(T * t, T * t + T)
                value = S[k, p, rows]
                edge = spread(s1, k, t, p)
                above = roll(jnp.where(first, edge, value), -1)
                below = roll(jnp.where(last, edge, value), 1)
                size = jnp.abs(value)
                a_above, a_below = jnp.abs(above), jnp.abs(below)
                for r in (rows,) if t else (low, high):
                    psi[k, p, r] = size
                    H[k, p, r] = 2.0 * size + (a_above + a_below)
                    O[k, p, r] = a_above - a_below
                    if k == 0:
                        SU[p, r] = above
                        SD[p, r] = below

    def window(w, dy):
        if w == 0:
            return slice(T + dy, T + dy + Y)
        return slice(Y + T - 1, Y + 2 * T - 1) if dy < 0 else slice(dy, T + dy)

    def rows_of(w):
        return slice(0, Y) if w == 0 else slice(Y, Y + T)

    for p in range(XX):
        for k in range(2):
            for w in range(2):
                A[k, p, rows_of(w)] = (
                    H[k, p, window(w, 0)] + psi[k, p, window(w, 1)] + psi[k, p, window(w, -1)]
                ) * (1.0 / 36.0)

    def gradient(k, p, w):
        gx = A[k, p + 1, rows_of(w)] - A[k, p - 1, rows_of(w)]
        ends = []
        for dy in (1, -1):
            r = window(w, dy)
            ends.append(H[k, p, r] + (psi[k, p + 1, r] + psi[k, p - 1, r]))
        gy = (ends[0] - ends[1]) * (1.0 / 36.0)
        r = window(w, 0)
        gz = 2.0 * O[k, p, r] + (O[k, p + 1, r] + O[k, p - 1, r])
        gz = (gz + (O[k, p, window(w, 1)] + O[k, p, window(w, -1)])) * (1.0 / 36.0)
        return gx, gy, gz

    def velocities(x, w):
        grads = [gradient(k, x + 2, w) for k in range(2)]
        common = [V[d, 1 + x, rows_of(w)] for d in range(3)]
        return [
            [common[d] - (COUPLING * RELAX[k]) * grads[1 - k][d] for d in range(3)]
            for k in range(2)
        ]

    def flat_of(u):
        return 1.0 - 1.5 * (u[0] * u[0] + u[1] * u[1] + u[2] * u[2])

    def one_way(w, flat, along, sign):
        even_part = w * (flat + 4.5 * (along * along))
        return even_part + w * ((3.0 * sign) * along)

    def collide_own(x):
        us = velocities(x, 0)
        for k in range(2):
            u = us[k]
            rho = psi[k, 2 + x, inner] * INV[k]
            flat = flat_of(u)
            scaled = {w: rho * w for w in sorted(set(WEIGHTS))}
            values = {0: scaled[WEIGHTS[0]] * flat}
            for i in range(1, 19, 2):
                along = along_of(i, u)
                w = scaled[WEIGHTS[i]]
                even_part = w * (flat + 4.5 * (along * along))
                odd_part = w * (3.0 * along)
                values[i] = even_part + odd_part
                values[i + 1] = even_part - odd_part
            for i in range(19):
                if abs(KEEP[k]) > 1e-9:
                    values[i] = values[i] + KEEP[k] * pop[k, i, x]
                post[k, i, 1 + x, inner] = values[i]

    row_sign = jnp.where(upper, -1.0, 1.0)

    def collide_rows(x):
        us = velocities(x, 1)
        for k in range(2):
            u = us[k]
            rho = psi[k, 2 + x, low] * INV[k]
            flat = flat_of(u)
            for m, i in enumerate(Y_UP):
                w = rho * WEIGHTS[i]
                value = one_way(w, flat, along_of(i, u), row_sign)
                if abs(KEEP[k]) > 1e-9:
                    value = value + KEEP[k] * WP[m, x]
                post[k, i, 1 + x, low] = value
                post[k, OPPOSITE[i], 1 + x, high] = value

    def collide_plane(n):
        x = -1 if n == 0 else X
        sign = 1.0 if n == 0 else -1.0
        us = velocities(x, 0)
        for k in range(2):
            u = us[k]
            rho = psi[k, 2 + x, inner] * INV[k]
            flat = flat_of(u)
            for m, i in enumerate(X_UP):
                value = one_way(rho * WEIGHTS[i], flat, along_of(i, u), sign)
                if abs(KEEP[k]) > 1e-9:
                    value = value + KEEP[k] * XP[n, m]
                post[k, i if n == 0 else OPPOSITE[i], 1 + x, inner] = value
        us = velocities(x, 1)
        cx = 1 if n == 0 else -1
        up, down = INDEX[(cx, 1, 0)], INDEX[(cx, -1, 0)]
        for k in range(2):
            u = us[k]
            rho = psi[k, 2 + x, low] * INV[k]
            value = one_way(rho * WEIGHTS[up], flat_of(u), sign * u[0] + row_sign * u[1], 1.0)
            if abs(KEEP[k]) > 1e-9:
                value = value + KEEP[k] * XPW[n]
            post[k, up, 1 + x, low] = value
            post[k, down, 1 + x, high] = value

    def collide_z():
        t1, t2 = gather_z(1)
        other1, other2 = roll(t1, HALF), roll(t2, HALF)
        lower = half == 0
        common = [
            jnp.where(lower, t1, other1),
            jnp.where(lower, t2, other2),
            jnp.where(lower, other1, t1),
        ]
        p0, p1, p2 = jnp.abs(s0), jnp.abs(s1), jnp.abs(s2)

        def x_up(v):
            return roll(v, -2)

        def x_down(v):
            return roll(v, 2)

        def y_up(v):
            r = roll_rows(v, -1)
            return jnp.where(row == T - 1, roll(r, -stride_t), r)

        def y_down(v):
            r = roll_rows(v, 1)
            return jnp.where(row == 0, roll(r, stride_t), r)

        xs = [x_up(v) + x_down(v) for v in (p0, p1, p2)]
        ys = [y_up(v) + y_down(v) for v in (p0, p1, p2)]
        g = 2.0 * p1 + (p0 + p2)
        a = g + ys[1]
        b = g + xs[1]
        c0 = 2.0 * p0 + (xs[0] + ys[0])
        c2 = 2.0 * p2 + (xs[2] + ys[2])
        sign = jnp.where(even, 1.0, -1.0)
        grads = [
            (x_up(a) - x_down(a)) * (1.0 / 36.0),
            (y_up(b) - y_down(b)) * (1.0 / 36.0),
            (c0 - c2) * (sign * (1.0 / 36.0)),
        ]
        factor = jnp.where(lower, COUPLING * RELAX[0], COUPLING * RELAX[1])
        u = [common[d] - factor * roll(grads[d], HALF) for d in range(3)]
        rho = p1 * jnp.where(lower, INV[0], INV[1])
        keep = jnp.where(lower, KEEP[0], KEEP[1])
        flat = flat_of(u)
        beyond = (slot < 2) | (slot >= X + 2)
        results = []
        for g, i in enumerate(Z_UP):
            p, h, b = POP_PLACE[g]
            old = roll(merged_z(0, p), 2 * (2 - b * X) + HALF * (1 - h))
            if VELOCITIES[i][0]:
                old = jnp.where(beyond, t2, old)
            value = one_way(rho * WEIGHTS[i], flat, along_of(i, u), sign)
            results.append(value + keep * jnp.where(lower, 0.0, old))
        for k in range(2):
            for g, i in enumerate(Z_UP):
                c = VELOCITIES[i]
                xs_needed = range(-1, X + 1) if c[0] else range(X)
                ts = range(YT + 2) if c[1] else range(1, YT + 1)
                for x in xs_needed:
                    for t in ts:
                        zpost[k, g, 1 + x, T * t:T * t + T] = spread(results[g], k, t, x + 2)

    def stream(x):
        fluid = solid[x] == 0
        for k in range(2):
            for i in range(19):
                c = VELOCITIES[i]
                rows = slice(T - c[1], T - c[1] + Y)
                read = post[k, i, 1 + x - c[0], rows]
                if i:
                    if c[2]:
                        edge = zpost[k, Z_PAIR[i], 1 + x - c[0], rows]
                        read = jnp.where(last_y if c[2] > 0 else first_y, edge, read)
                        read = roll(read, c[2])
                    p = 2 + x - c[0]
                    source = (SD if c[2] > 0 else SU)[p, rows] if c[2] else S[0, p, rows]
                    bounced = post[k, OPPOSITE[i], 1 + x, inner]
                    read = jnp.where(source > 0.0, read, bounced)
                out[k, i, x] = jnp.where(fluid, read, pop[k, i, x])

    for x in range(X):
        collide_own(x)
    for x in range(X):
        collide_rows(x)
    collide_z()
    for x in range(1, X - 1):
        stream(x)
    await_("xV")
    await_("xP")
    for n in range(2):
        plane = 0 if n == 0 else X + 1
        tile = XWR[n, 2]
        for d in range(3):
            V[d, plane, Y:Y + T] = roll_rows(tile, -2 * d)
        XPW[n] = roll_rows(tile, -6)
    for n in range(2):
        collide_plane(n)
    for x in (0, X - 1):
        stream(x)
    for copy in copies.values():
        copy.wait_send()


def body(populations, solid):
    X, Y, Z = solid.shape
    f32 = jnp.float32
    dma = pltpu.SemaphoreType.DMA
    R = Y + 2 * T

    def vmem(*shape):
        return pltpu.VMEM(shape, f32)

    return pl.pallas_call(
        step_kernel,
        out_shape=pltpu.VMEM(populations.shape, f32),
        in_specs=[pl.BlockSpec(memory_space=pl.ANY)] * 2,
        out_specs=pl.BlockSpec(memory_space=pltpu.VMEM),
        scratch_shapes=[
            vmem(*populations.shape),
            pltpu.VMEM(solid.shape, jnp.int32),
            vmem(2, X + 4, R, Z),
            vmem(X + 4, R, Z),
            vmem(X + 4, R, Z),
            vmem(2, X + 4, R, Z),
            vmem(2, X + 4, R, Z),
            vmem(2, X + 4, R, Z),
            vmem(2, X + 4, Y + T, Z),
            vmem(3, X + 2, Y + T, Z),
            vmem(2, 19, X + 2, R, Z),
            vmem(2, 5, X + 2, R, Z),
            vmem(2, 2, X, T, Z),
            vmem(2, 3, X, T, Z),
            vmem(2, 5, X, T, Z),
            vmem(5, X, T, Z),
            vmem(2, 5, Y, Z),
            vmem(2, 3, T, Z),
            vmem(2, 3, T, Z),
            vmem(2, T, Z),
            vmem(4, T, LANES),
            vmem(2, T, LANES),
            vmem(6, 4, T, LANES),
            dma((X + 1,)),
            dma((38,)),
            dma((38,)),
            pltpu.SemaphoreType.REGULAR,
            pltpu.SemaphoreType.REGULAR,
        ],
        compiler_params=pltpu.CompilerParams(collective_id=0, has_side_effects=True),
    )(populations, solid)


def solution(mesh):
    in_specs = (P(None, None, "gx", "gy", "gz"), P("gx", "gy", "gz"))
    out_specs = P(None, None, "gx", "gy", "gz")
    return jax.shard_map(body, mesh=mesh, in_specs=in_specs, out_specs=out_specs, check_vma=False)
```

time: 19.1 us -> 15.9 us (0.83)
  Pallas kernels: 17.9 us -> 14.7 us
    pallas_call x1, Pallas kernels: 17.9 us -> 14.7 us  [body(): pl.pallas_call(step_kernel, out_shape=pltpu.VMEM(populations.shape, f32),...]
where the time goes in v1:
time: 15.9 us; the launch traced here: 15.7 us
  Pallas kernels  14.7 us (92%)
  local copies, waits for them, and re-layouts  1.04 us (7%)
    pallas_call x1, Pallas kernels, body(): pl.pallas_call(step_kernel, out_shape=pltpu.VMEM(populations.shape, f32),...  14.7 us
    unnamed x1, local copies, waits for them, and re-layouts  1.04 us

profile of v1, /device:TPU:0, one launch (start us, length us, event | category | flops | bytes accessed | tf_op | source)
XLA Modules:
  0.0 15.7 jit_solution(3845976464740405636)
XLA Ops:
  0.0 14.7 %shard_map.28 = f32[2,19,4,16,128]{4,3,2,1,0:T(8,128)S(1)} custom-call(f32[2,19,4,16,128]{4,3,2,1,0:T(8,128)} %pop_hbm.1, s32[4,16,128]{2,1,0:T(8,128)} %solid_hbm.1), custom_call_target="tpu_custom_call" | custom-call | tf_op jit(solution)/shard_map/pallas_call | solution.py:570
  14.7 1.0 %copy.4 = f32[2,19,4,16,128]{4,3,2,1,0:T(8,128)} copy(f32[2,19,4,16,128]{4,3,2,1,0:T(8,128)S(1)} %shard_map.28) | data formatting | bytes 2490368

commit v2 on v1

v2 whole, which is shorter than its diff:
```python
import jax
import jax.numpy as jnp
from jax import lax
from jax.experimental import pallas as pl
from jax.experimental.pallas import tpu as pltpu
from jax.sharding import PartitionSpec as P

VELOCITIES = [
    (0, 0, 0),
    (1, 0, 0),
    (-1, 0, 0),
    (0, 1, 0),
    (0, -1, 0),
    (0, 0, 1),
    (0, 0, -1),
    (1, 1, 0),
    (-1, -1, 0),
    (1, -1, 0),
    (-1, 1, 0),
    (1, 0, 1),
    (-1, 0, -1),
    (1, 0, -1),
    (-1, 0, 1),
    (0, 1, 1),
    (0, -1, -1),
    (0, 1, -1),
    (0, -1, 1),
]
WEIGHTS = [1.0 / 3.0] + [1.0 / 18.0] * 6 + [1.0 / 36.0] * 12
OPPOSITE = [0, 2, 1, 4, 3, 6, 5, 8, 7, 10, 9, 12, 11, 14, 13, 16, 15, 18, 17]
INDEX = {v: i for i, v in enumerate(VELOCITIES)}
COUPLING = 0.9
RELAX = (1.0, 0.8)
WALL = (0.3, 1.5)
INV = [1.0 / t for t in RELAX]
KEEP = [1.0 - v for v in INV]
AXES = ("gx", "gy", "gz")
MESH = pl.DeviceIdType.MESH

X_UP = [i for i in range(19) if VELOCITIES[i][0] == 1]
Y_UP = [i for i in range(19) if VELOCITIES[i][1] == 1]
Z_UP = [(0, 0, 1), (1, 0, 1), (-1, 0, 1), (0, 1, 1), (0, -1, 1)]
Z_UP = [INDEX[v] for v in Z_UP]
Z_PAIR = {}
for _g, _i in enumerate(Z_UP):
    Z_PAIR[_i] = _g
    Z_PAIR[OPPOSITE[_i]] = _g
Z_FROM = [(dx, dz) for dz in (-1, 1) for dx in (0, -1, 1)]
T = 8
LANES = 128
HALF = LANES // 2


def along_of(i, u):
    total = None
    for d in range(3):
        c = VELOCITIES[i][d]
        if c:
            term = u[d] if c > 0 else -u[d]
            total = term if total is None else total + term
    return total


def step_kernel(pop_hbm, solid_hbm, out, pop, solid, S, SU, SD, psi, H, O, A, V, post, zpost,
                YR, WP, XB, XWP, XSND, XE, ZS, YW, ZF, ZD, tally, load_sem, send_sem, recv_sem,
                near_sem, far_sem):
    X, Y, Z = solid.shape
    YT = Y // T
    inner = slice(T, T + Y)
    low, high = slice(0, T), slice(Y + T, Y + 2 * T)
    XX = X + 4
    stride_t = HALF // (YT + 2)
    assert Z == LANES and YT == 2 and X >= 3
    assert stride_t >= 2 * XX and 2 * X <= XX

    me = [lax.axis_index(a) for a in AXES]
    count = [lax.axis_size(a) for a in AXES]
    assert count[1] % 2 == 0
    y_sides = (1,) if count[1] == 2 else (1, -1)
    NY = len(y_sides)
    y_slot = {1: 0, -1: NY - 1}

    loads = [pltpu.make_async_copy(solid_hbm, solid, load_sem.at[0])]
    cuts = [0, X // 2, X]
    for n in range(2):
        part = slice(cuts[n], cuts[n + 1])
        loads.append(
            pltpu.make_async_copy(pop_hbm.at[:, :, part], pop.at[:, :, part], load_sem.at[1 + n])
        )
    for copy in loads:
        copy.start()

    parity = lax.rem(me[1], 2)
    is_near, is_far = parity == 0, parity == 1

    def device(offset):
        return tuple(lax.rem(me[d] + offset[d] + count[d], count[d]) for d in range(3))

    barrier = pltpu.get_barrier_semaphore()
    partner = (me[0], me[1] + 1 - 2 * parity, me[2])
    pairs = [me[1] - parity]
    if count[1] > 2:
        pairs.append(lax.rem(me[1] + 3 * parity - 2 + count[1], count[1]))

    def arrive(place):
        pl.semaphore_signal(barrier, inc=1, device_id=place, device_id_type=MESH)

    for dx in (1, -1, 0):
        for dz in (1, -1):
            place = device((dx, 0, dz))
            for base in pairs:
                arrive((place[0], base + 1, place[2]))
    for dx in (1, -1):
        place = device((dx, 0, 0))
        for base in pairs:
            arrive((place[0], base, place[2]))
    for base in pairs[1:]:
        arrive((me[0], base, me[2]))
    arrive(partner)
    near_count, far_count = 4 + 1, 12 + 1
    if count[1] > 2:
        near_count, far_count = near_count + 6, far_count + 12

    lane = lax.broadcasted_iota(jnp.int32, (T, LANES), 1)
    row = lax.broadcasted_iota(jnp.int32, (T, LANES), 0)
    pair = lane // 2
    even = lane % 2 == 0
    half = lane // HALF
    lower = half == 0
    slot = (lane % stride_t) // 2
    tile_t = (lane % HALF) // stride_t
    own_t = (tile_t > 0) & (tile_t <= YT)
    first, last = lane == 0, lane == Z - 1
    lane_y = lax.broadcasted_iota(jnp.int32, (Y, LANES), 1)
    first_y, last_y = lane_y == 0, lane_y == Z - 1
    upper = row < T // 2

    def roll(v, n):
        n = n % LANES
        return pltpu.roll(v, n, 1) if n else v

    def roll_rows(v, n):
        n = n % T
        return pltpu.roll(v, n, 0) if n else v

    def swap(v):
        return jnp.where(even, roll(v, -1), roll(v, 1))

    GROUPS = {"y": 0, "yW": 1, "xS": 2, "xE": 3, "zF": 4, "zD": 5, "xB": 6}
    sent = [0]

    def send(group, src, dst, offset, tiles):
        pltpu.make_async_remote_copy(
            src_ref=src,
            dst_ref=dst,
            send_sem=send_sem,
            recv_sem=recv_sem.at[GROUPS[group]],
            device_id=device(offset),
            device_id_type=MESH,
        ).start()
        sent[0] += tiles

    def await_(group, ref):
        pltpu.make_async_copy(ref, ref, recv_sem.at[GROUPS[group]]).wait()

    @pl.when(is_near)
    def _():
        pl.semaphore_wait(barrier, near_count)
        pl.semaphore_signal(near_sem, inc=1, device_id=partner, device_id_type=MESH)

    def moments(x):
        fluid = solid[x] == 0
        total, mom = [], []
        for k in range(2):
            f = [pop[k, i, x] for i in range(19)]
            rho = f[0]
            m = [None, None, None]
            for i in range(1, 19, 2):
                rho = rho + (f[i] + f[i + 1])
                diff = f[i] - f[i + 1]
                for d in range(3):
                    c = VELOCITIES[i][d]
                    if c:
                        m[d] = (
                            (diff if c > 0 else -diff)
                            if m[d] is None
                            else (m[d] + diff if c > 0 else m[d] - diff)
                        )
            total.append(rho)
            S[k, 2 + x, inner] = jnp.where(fluid, rho, -WALL[k])
            mom.append([v * INV[k] if INV[k] != 1.0 else v for v in m])
        scale = 1.0 / (total[0] * INV[0] + total[1] * INV[1])
        for d in range(3):
            V[d, 1 + x, 0:Y] = (mom[0][d] + mom[1][d]) * scale

    loads[0].wait()
    for n in range(2):
        loads[1 + n].wait()
        for x in range(cuts[n], cuts[n + 1]):
            moments(x)

    @pl.when(is_far)
    def _():
        pl.semaphore_wait(near_sem, 1)

    first_up = lax.rem(me[0], 4) != 1
    sides = [jnp.where(first_up, 1, -1), jnp.where(first_up, -1, 1)]

    def send_x_signs(side):
        up = side > 0
        src = jnp.where(up, X, 2)
        dst = jnp.where(up, 0, X + 2)
        send("xS", S.at[:, pl.ds(src, 2), inner], S.at[:, pl.ds(dst, 2), inner],
             (side, 0, 0), 4 * YT)

    def send_x_bulk(side):
        up = side > 0
        n = jnp.where(up, 0, 1)
        to = (side, 0, 0)
        send("xB", V.at[:, jnp.where(up, X, 1), 0:Y], XB.at[n, 0:3], to, 3 * YT)
        for m, i in enumerate(X_UP):
            send("xB", pop.at[1, jnp.where(up, i, OPPOSITE[i]), jnp.where(up, X - 1, 0)],
                 XB.at[n, 3 + m], to, YT)

    send_x_signs(sides[0])
    for n, side in enumerate((1, -1)):
        tile = slice(Y - T, Y) if side > 0 else slice(0, T)
        wide = slice(Y, Y + T) if side > 0 else slice(T, 2 * T)
        to = (0, side, 0)
        send("y", S.at[:, 2:2 + X, wide], YR.at[n, 0:2], to, 2 * X)
        send("y", V.at[:, 1:1 + X, tile], YR.at[n, 2:5], to, 3 * X)
        for m, i in enumerate(Y_UP):
            i = i if side > 0 else OPPOSITE[i]
            send("y", pop.at[1, i, :, tile], YR.at[n, 5 + m], to, X)

    blank = jnp.zeros((T, LANES), jnp.float32)
    packs = [blank, blank, blank, blank]
    POP_PLACE = [(2, 0, 0), (2, 0, 1), (2, 1, 0), (2, 1, 1), (3, 1, 0)]
    V_PLACE = [(1, 0, 0), (1, 0, 1), (1, 1, 0)]

    def put(p, h, b, t, x, value):
        j = (h * HALF + t * stride_t + (b * X + x) * 2) // 2
        packs[p] = jnp.where(pair == j, roll(value, 2 * j + 1), packs[p])

    for x in range(X):
        for t in range(1, YT + 1):
            rows = slice(T * t, T * t + T)
            rows_v = slice(T * (t - 1), T * t)
            for k in range(2):
                value = S[k, 2 + x, rows]
                put(0, k, 0, t, x, value)
                put(0, k, 1, t, x, jnp.where(lane < HALF, roll(value, -1), roll(value, 1)))
            for d in range(3):
                put(*V_PLACE[d], t, x, V[d, 1 + x, rows_v])
            for g, i in enumerate(Z_UP):
                value = jnp.where(lane < HALF, pop[1, OPPOSITE[i], x, rows_v], pop[1, i, x, rows_v])
                put(*POP_PLACE[g], t, x, value)
    place = slot % X
    diag = jnp.where((place == X - 1) == even, roll(packs[2], HALF), roll(packs[2], 2 * X))
    packs[1] = jnp.where((half == 1) & (slot >= X) & (slot < 2 * X), diag, packs[1])

    def edges(v, q):
        return jnp.where(upper, roll(v, (q - 1) * stride_t), roll(v, (q - YT) * stride_t))

    merged = edges(packs[0], 0)
    for p in range(1, 4):
        merged = jnp.where(tile_t == p, edges(packs[p], p), merged)
    for p in range(4):
        ZS[p] = packs[p]
    ZS[4] = merged
    for n in range(2):
        if n == 0:
            tile = jnp.where(place >= X - 2, packs[0], roll(packs[1], -2 * (X - 1)))
        else:
            tile = jnp.where(place < 2, packs[0], roll(packs[1], 2 * (X - 1)))
        XSND[n, 0] = jnp.where(tile_t == 0, edges(tile, 0), tile)

    def ends(a, b):
        return jnp.where(upper, a, b)

    t_first, t_last = slice(0, T), slice(Y - T, Y)
    s_first, s_last = slice(T, 2 * T), slice(Y, Y + T)
    keep_rows = (row < 2) | (row >= T - 2)
    for n, side in enumerate((1, -1)):
        planes = (X, X + 1) if side > 0 else (2, 3)
        for m, p in enumerate(planes):
            both = [ends(S[k, p, s_first], S[k, p, s_last]) for k in range(2)]
            XSND[n, 1 + m] = jnp.where(keep_rows, both[0], roll_rows(both[1], 4))
        x = X - 1 if side > 0 else 0
        up, down = INDEX[(side, 1, 0)], INDEX[(side, -1, 0)]
        fields = [ends(V[d, 1 + x, t_first], V[d, 1 + x, t_last]) for d in range(3)]
        fields.append(ends(pop[1, down, x, t_first], pop[1, up, x, t_last]))
        packed = fields[0]
        for f in range(1, 4):
            at = (row == 2 * f - 1) | (row == 2 * f)
            packed = jnp.where(at, roll_rows(fields[f], 2 * f), packed)
        XSND[n, 3] = packed

    for n, side in enumerate((1, -1)):
        send("xE", XSND.at[n, 0:1], XE.at[n, 0:1], (side, 0, 0), 1)
        for sy in y_sides:
            m = 1 + 4 * y_slot[-sy]
            send("xE", XSND.at[n], XE.at[n, m:m + 4], (side, sy, 0), 4)
    for sy in y_sides:
        send("yW", ZS.at[4], YW.at[y_slot[-sy]], (0, sy, 0), 1)
    send_x_bulk(sides[0])
    send_x_signs(sides[1])
    send_x_bulk(sides[1])

    @pl.when(is_far)
    def _():
        pl.semaphore_wait(barrier, far_count)
        pl.semaphore_signal(far_sem, inc=1, device_id=partner, device_id_type=MESH)

    @pl.when(is_near)
    def _():
        pl.semaphore_wait(far_sem, 1)

    for n, side in enumerate((1, -1)):
        for m, dz in enumerate((1, -1)):
            send("zD", XSND.at[n, 0], ZD.at[m, n, 0], (side, 0, dz), 1)
            for sy in y_sides:
                send("zD", XSND.at[n, 0], ZD.at[m, n, 1 + y_slot[-sy]], (side, sy, dz), 1)
    for m, dz in enumerate((1, -1)):
        send("zF", ZS.at[0:4], ZF.at[m, 0:4], (0, 0, dz), 4)
        for sy in y_sides:
            send("zF", ZS.at[4], ZF.at[m, 4 + y_slot[-sy]], (0, sy, dz), 1)

    await_("y", YR)
    for x in range(X):
        for k in range(2):
            value = ends(YR[1, k, x], YR[0, k, x])
            S[k, 2 + x, low] = value
            S[k, 2 + x, high] = value
        for d in range(3):
            V[d, 1 + x, Y:Y + T] = ends(YR[1, 2 + d, x], YR[0, 2 + d, x])
        for m in range(5):
            WP[m, x] = ends(YR[1, 5 + m, x], YR[0, 5 + m, x])

    def window(w, dy):
        if w == 0:
            return slice(T + dy, T + dy + Y)
        return slice(Y + T - 1, Y + 2 * T - 1) if dy < 0 else slice(dy, T + dy)

    def rows_of(w):
        return slice(0, Y) if w == 0 else slice(Y, Y + T)

    def prepare(p):
        for k in range(2):
            for t in range(YT + 1):
                rows = slice(T * t, T * t + T)
                value = S[k, p, rows]
                SU[k, p, rows] = roll(value, -1)
                SD[k, p, rows] = roll(value, 1)

    def spread(tile, k, t, xx):
        return roll(tile, LANES - 1 - (k * HALF + t * stride_t + 2 * xx))

    def complete(p, signs):
        for k in range(2):
            for t in range(YT + 1):
                rows = slice(T * t, T * t + T)
                edge = spread(signs, k, t, p)
                above = jnp.where(last, edge, SU[k, p, rows])
                below = jnp.where(first, edge, SD[k, p, rows])
                size = jnp.abs(S[k, p, rows])
                a_above, a_below = jnp.abs(above), jnp.abs(below)
                for r in (rows,) if t else (low, high):
                    psi[k, p, r] = size
                    H[k, p, r] = 2.0 * size + (a_above + a_below)
                    O[k, p, r] = a_above - a_below
                    if k == 0:
                        SU[k, p, r] = above
                        SD[k, p, r] = below

    def sums(p):
        for k in range(2):
            for w in range(2):
                A[k, p, rows_of(w)] = (
                    H[k, p, window(w, 0)] + (psi[k, p, window(w, 1)] + psi[k, p, window(w, -1)])
                ) * (1.0 / 36.0)

    def gradient(k, p, w):
        gx = A[k, p + 1, rows_of(w)] - A[k, p - 1, rows_of(w)]
        sides_y = []
        for dy in (1, -1):
            r = window(w, dy)
            sides_y.append(H[k, p, r] + (psi[k, p + 1, r] + psi[k, p - 1, r]))
        gy = (sides_y[0] - sides_y[1]) * (1.0 / 36.0)
        r = window(w, 0)
        gz = 2.0 * O[k, p, r] + (O[k, p + 1, r] + O[k, p - 1, r])
        gz = (gz + (O[k, p, window(w, 1)] + O[k, p, window(w, -1)])) * (1.0 / 36.0)
        return gx, gy, gz

    def velocities(common, x, w):
        grads = [gradient(k, x + 2, w) for k in range(2)]
        return [
            [common[d] - (COUPLING * RELAX[k]) * grads[1 - k][d] for d in range(3)]
            for k in range(2)
        ]

    def common_of(x, w):
        return [V[d, 1 + x, rows_of(w)] for d in range(3)]

    def flat_of(u):
        return 1.0 - 1.5 * (u[0] * u[0] + u[1] * u[1] + u[2] * u[2])

    def one_way(w, flat, along, sign):
        even_part = w * (flat + 4.5 * (along * along))
        return even_part + w * ((3.0 * sign) * along)

    def collide_own(x):
        us = velocities(common_of(x, 0), x, 0)
        for k in range(2):
            u = us[k]
            rho = psi[k, 2 + x, inner] * INV[k]
            flat = flat_of(u)
            scaled = {w: rho * w for w in sorted(set(WEIGHTS))}
            values = {0: scaled[WEIGHTS[0]] * flat}
            for i in range(1, 19, 2):
                along = along_of(i, u)
                w = scaled[WEIGHTS[i]]
                even_part = w * (flat + 4.5 * (along * along))
                odd_part = w * (3.0 * along)
                values[i] = even_part + odd_part
                values[i + 1] = even_part - odd_part
            for i in range(19):
                if abs(KEEP[k]) > 1e-9:
                    values[i] = values[i] + KEEP[k] * pop[k, i, x]
                post[k, i, 1 + x, inner] = values[i]

    row_sign = jnp.where(upper, -1.0, 1.0)

    def collide_rows(x):
        us = velocities(common_of(x, 1), x, 1)
        for k in range(2):
            u = us[k]
            rho = psi[k, 2 + x, low] * INV[k]
            flat = flat_of(u)
            for m, i in enumerate(Y_UP):
                w = rho * WEIGHTS[i]
                value = one_way(w, flat, along_of(i, u), row_sign)
                if abs(KEEP[k]) > 1e-9:
                    value = value + KEEP[k] * WP[m, x]
                post[k, i, 1 + x, low] = value
                post[k, OPPOSITE[i], 1 + x, high] = value

    def collide_plane(n):
        x = -1 if n == 0 else X
        sign = 1.0 if n == 0 else -1.0
        us = velocities([XB[n, d] for d in range(3)], x, 0)
        for k in range(2):
            u = us[k]
            rho = psi[k, 2 + x, inner] * INV[k]
            flat = flat_of(u)
            for m, i in enumerate(X_UP):
                value = one_way(rho * WEIGHTS[i], flat, along_of(i, u), sign)
                if abs(KEEP[k]) > 1e-9:
                    value = value + KEEP[k] * XB[n, 3 + m]
                post[k, i if n == 0 else OPPOSITE[i], 1 + x, inner] = value

    def collide_corner(n):
        x = -1 if n == 0 else X
        sign = 1.0 if n == 0 else -1.0
        us = velocities(common_of(x, 1), x, 1)
        cx = 1 if n == 0 else -1
        up, down = INDEX[(cx, 1, 0)], INDEX[(cx, -1, 0)]
        for k in range(2):
            u = us[k]
            rho = psi[k, 2 + x, low] * INV[k]
            value = one_way(rho * WEIGHTS[up], flat_of(u), sign * u[0] + row_sign * u[1], 1.0)
            if abs(KEEP[k]) > 1e-9:
                value = value + KEEP[k] * XWP[n]
            post[k, up, 1 + x, low] = value
            post[k, down, 1 + x, high] = value

    def x_up(v):
        return roll(v, -2)

    def x_down(v):
        return roll(v, 2)

    def y_up(v):
        r = roll_rows(v, -1)
        return jnp.where(row == T - 1, roll(r, -stride_t), r)

    def y_down(v):
        r = roll_rows(v, 1)
        return jnp.where(row == 0, roll(r, stride_t), r)

    def collide_z(s0, s1, s2, t1, t2, olds):
        other1, other2 = roll(t1, HALF), roll(t2, HALF)
        common = [
            jnp.where(lower, t1, other1),
            jnp.where(lower, t2, other2),
            jnp.where(lower, other1, t1),
        ]
        p0, p1, p2 = jnp.abs(s0), jnp.abs(s1), jnp.abs(s2)
        xs = [x_up(v) + x_down(v) for v in (p0, p1, p2)]
        ys = [y_up(v) + y_down(v) for v in (p0, p1, p2)]
        g = 2.0 * p1 + (p0 + p2)
        a = g + ys[1]
        b = g + xs[1]
        c0 = 2.0 * p0 + (xs[0] + ys[0])
        c2 = 2.0 * p2 + (xs[2] + ys[2])
        sign = jnp.where(even, 1.0, -1.0)
        grads = [
            (x_up(a) - x_down(a)) * (1.0 / 36.0),
            (y_up(b) - y_down(b)) * (1.0 / 36.0),
            (c0 - c2) * (sign * (1.0 / 36.0)),
        ]
        factor = jnp.where(lower, COUPLING * RELAX[0], COUPLING * RELAX[1])
        u = [common[d] - factor * roll(grads[d], HALF) for d in range(3)]
        rho = p1 * jnp.where(lower, INV[0], INV[1])
        keep = jnp.where(lower, KEEP[0], KEEP[1])
        flat = flat_of(u)
        beyond = (slot < 2) | (slot >= X + 2)
        for g, i in enumerate(Z_UP):
            c = VELOCITIES[i]
            old = jnp.where(beyond, t2, olds[g]) if c[0] else olds[g]
            value = one_way(rho * WEIGHTS[i], flat, along_of(i, u), sign)
            value = value + keep * jnp.where(lower, 0.0, old)
            if c[0]:
                value = jnp.where(even, roll(value, 2 * c[0]), roll(value, -2 * c[0]))
            if c[1]:
                a, b = (y_down, y_up) if c[1] > 0 else (y_up, y_down)
                value = jnp.where(even, a(value), b(value))
            value = swap(value)
            for k in range(2):
                for x in range(X):
                    for t in range(1, YT + 1):
                        zpost[k, g, x, T * (t - 1):T * t] = spread(value, k, t, x + 2)

    def stream(x):
        fluid = solid[x] == 0
        for k in range(2):
            for i in range(19):
                c = VELOCITIES[i]
                rows = slice(T - c[1], T - c[1] + Y)
                read = post[k, i, 1 + x - c[0], rows]
                if i:
                    if c[2]:
                        at = first_y if c[2] > 0 else last_y
                        read = jnp.where(at, zpost[k, Z_PAIR[i], x], roll(read, c[2]))
                    p = 2 + x - c[0]
                    signs = SD if c[2] > 0 else (SU if c[2] else S)
                    bounced = post[k, OPPOSITE[i], 1 + x, inner]
                    read = jnp.where(signs[0, p, rows] > 0.0, read, bounced)
                out[k, i, x] = jnp.where(fluid, read, pop[k, i, x])

    for x in range(X):
        prepare(2 + x)

    def with_rows(tile, w_low, w_high):
        return jnp.where(own_t, tile, jnp.where(tile_t == 0, w_low, w_high))

    def by_row(low_part, high_part):
        return low_part if NY == 1 else ends(low_part, high_part)

    top = stride_t * (YT + 1)

    await_("zF", ZF)
    faces = [jnp.where(even, ZF[0, p], ZF[1, p]) for p in range(4 + NY)]
    z_rows = by_row(faces[4 + y_slot[1]], faces[4 + y_slot[-1]])
    full = [
        with_rows(faces[p], roll(z_rows, -stride_t * p), roll(z_rows, top - stride_t * p))
        for p in range(4)
    ]
    center = [[roll(full[p], 2 * (2 - b * X)) for b in range(2)] for p in range(2)]
    olds = []
    for p, h, b in POP_PLACE:
        olds.append(roll(full[p], 2 * (2 - b * X) + HALF * (1 - h)))
    near_signs = swap(center[0][0])
    for x in range(X):
        complete(2 + x, near_signs)
    for x in range(X):
        sums(2 + x)
    for x in range(1, X - 1):
        collide_own(x)
        collide_rows(x)

    await_("yW", YW)
    await_("xS", S.at[:, 0:4, inner])
    await_("xE", XE)
    for n in range(2):
        planes = (0, 1) if n == 0 else (X + 2, X + 3)
        ups, downs = 1 + 4 * y_slot[1], 1 + 4 * y_slot[-1]
        for m, p in enumerate(planes):
            value = XE[n, ups + 1 + m]
            if NY > 1:
                value = jnp.where(row % 4 < 2, value, XE[n, downs + 1 + m])
            other = roll_rows(value, 4)
            for k, w in ((0, value), (1, other)):
                S[k, p, low] = w
                S[k, p, high] = w
        value = XE[n, ups + 3]
        if NY > 1:
            value = jnp.where(row % 2 == 0, value, XE[n, downs + 3])
        plane = 0 if n == 0 else X + 1
        for d in range(3):
            V[d, plane, Y:Y + T] = roll_rows(value, -2 * d)
        XWP[n] = roll_rows(value, -6)
    outer = [0, 1, X + 2, X + 3]
    for p in outer:
        prepare(p)

    def assemble(middle, left, right, shift_left, shift_right):
        return jnp.where(
            slot < 2,
            roll(left, 2 * shift_left),
            jnp.where(slot >= X + 2, roll(right, 2 * shift_right), middle),
        )

    y_rows = by_row(YW[y_slot[1]], YW[y_slot[-1]])
    own = with_rows(ZS[0], y_rows, roll(y_rows, top))
    beside = []
    for n in range(2):
        w = by_row(XE[n, 1 + 4 * y_slot[1]], XE[n, 1 + 4 * y_slot[-1]])
        beside.append(with_rows(XE[n, 0], w, roll(w, top)))
    s0 = swap(assemble(roll(own, 4), beside[0], beside[1], 2 - X, X + 2))

    await_("zD", ZD)
    diags = []
    for n in range(2):
        merged = [jnp.where(even, ZD[0, n, q], ZD[1, n, q]) for q in range(1 + NY)]
        w = by_row(merged[1 + y_slot[1]], merged[1 + y_slot[-1]])
        diags.append(with_rows(merged[0], w, roll(w, top)))
    s1, s2 = [
        assemble(center[0][b], *diags, -(b * X + X - 2), X + 2 - b * X) for b in range(2)
    ]
    t1, t2 = [assemble(center[1][b], *diags, 1 - b * X, 3 - b * X) for b in range(2)]
    signs = swap(s1)
    for p in outer:
        complete(p, signs)
    for p in outer:
        sums(p)
    for x in (0, X - 1):
        collide_own(x)
        collide_rows(x)
    collide_z(s0, s1, s2, t1, t2, olds)
    for n in range(2):
        collide_corner(n)
    for x in range(1, X - 1):
        stream(x)
    await_("xB", XB)
    for n in range(2):
        collide_plane(n)
    for x in (0, X - 1):
        stream(x)
    assert sent[0] == tally.shape[0]
    pltpu.make_async_copy(tally, tally, send_sem).wait()


def body(populations, solid):
    X, Y, Z = solid.shape
    f32 = jnp.float32
    dma = pltpu.SemaphoreType.DMA
    R = Y + 2 * T
    XX = X + 4
    NY = 1 if lax.axis_size("gy") == 2 else 2
    YT = Y // T
    tiles = 20 * X + 24 * YT + 14 + 15 * NY

    def vmem(*shape):
        return pltpu.VMEM(shape, f32)

    return pl.pallas_call(
        step_kernel,
        out_shape=pltpu.VMEM(populations.shape, f32),
        in_specs=[pl.BlockSpec(memory_space=pl.ANY)] * 2,
        out_specs=pl.BlockSpec(memory_space=pltpu.VMEM),
        scratch_shapes=[
            vmem(*populations.shape),
            pltpu.VMEM(solid.shape, jnp.int32),
            vmem(2, XX, R, Z),
            vmem(2, XX, R, Z),
            vmem(2, XX, R, Z),
            vmem(2, XX, R, Z),
            vmem(2, XX, R, Z),
            vmem(2, XX, R, Z),
            vmem(2, XX, Y + T, Z),
            vmem(3, X + 2, Y + T, Z),
            vmem(2, 19, X + 2, R, Z),
            vmem(2, 5, X, Y, Z),
            vmem(2, 10, X, T, Z),
            vmem(5, X, T, Z),
            vmem(2, 8, Y, Z),
            vmem(2, T, Z),
            vmem(2, 4, T, LANES),
            vmem(2, 1 + 4 * NY, T, LANES),
            vmem(5, T, LANES),
            vmem(NY, T, LANES),
            vmem(2, 4 + NY, T, LANES),
            vmem(2, 2, 1 + NY, T, LANES),
            vmem(tiles, T, LANES),
            dma((3,)),
            dma,
            dma((7,)),
            pltpu.SemaphoreType.REGULAR,
            pltpu.SemaphoreType.REGULAR,
        ],
        compiler_params=pltpu.CompilerParams(collective_id=0, has_side_effects=True),
    )(populations, solid)


def solution(mesh):
    in_specs = (P(None, None, "gx", "gy", "gz"), P("gx", "gy", "gz"))
    out_specs = P(None, None, "gx", "gy", "gz")
    return jax.shard_map(body, mesh=mesh, in_specs=in_specs, out_specs=out_specs, check_vma=False)
```

time: 15.9 us -> 13.8 us (0.87)
  Pallas kernels: 14.7 us -> 12.7 us
    pallas_call x1, Pallas kernels: 14.7 us -> 12.7 us  [body(): pl.pallas_call(step_kernel, out_shape=pltpu.VMEM(populations.shape, f32),...]
where the time goes in v2:
time: 13.8 us; the launch traced here: 13.7 us
  Pallas kernels  12.7 us (92%)
  local copies, waits for them, and re-layouts  1.04 us (8%)
    pallas_call x1, Pallas kernels, body(): pl.pallas_call(step_kernel, out_shape=pltpu.VMEM(populations.shape, f32),...  12.7 us
    unnamed x1, local copies, waits for them, and re-layouts  1.04 us

profile of v2, /device:TPU:0, one launch (start us, length us, event | category | flops | bytes accessed | tf_op | source)
XLA Modules:
  0.0 13.7 jit_solution(13502133474166326122)
XLA Ops:
  0.0 12.7 %shard_map.28 = f32[2,19,4,16,128]{4,3,2,1,0:T(8,128)S(1)} custom-call(f32[2,19,4,16,128]{4,3,2,1,0:T(8,128)} %pop_hbm.1, s32[4,16,128]{2,1,0:T(8,128)} %solid_hbm.1), custom_call_target="tpu_custom_call" | custom-call | tf_op jit(solution)/shard_map/pallas_call | solution.py:667
  12.7 1.0 %copy.4 = f32[2,19,4,16,128]{4,3,2,1,0:T(8,128)} copy(f32[2,19,4,16,128]{4,3,2,1,0:T(8,128)S(1)} %shard_map.28) | data formatting | bytes 2490368

commit v3 on v2

--- a/solution.py
+++ b/solution.py
@@ -163,11 +163,6 @@
     def await_(group, ref):
         pltpu.make_async_copy(ref, ref, recv_sem.at[GROUPS[group]]).wait()
 
-    @pl.when(is_near)
-    def _():
-        pl.semaphore_wait(barrier, near_count)
-        pl.semaphore_signal(near_sem, inc=1, device_id=partner, device_id_type=MESH)
-
     def moments(x):
         fluid = solid[x] == 0
         total, mom = [], []
@@ -193,81 +188,50 @@
         for d in range(3):
             V[d, 1 + x, 0:Y] = (mom[0][d] + mom[1][d]) * scale
 
+    blank = jnp.zeros((T, LANES), jnp.float32)
+    packs = [blank, blank, blank, blank]
+    POP_PLACE = [(2, 0, 0), (2, 0, 1), (2, 1, 0), (2, 1, 1), (3, 1, 0)]
+    V_PLACE = [(1, 0, 0), (1, 0, 1), (1, 1, 0)]
+
+    def put(p, h, b, t, x, value, inside=False):
+        j = (h * HALF + t * stride_t + (b * X + x) * 2) // 2
+        if inside:
+            value = jnp.where(even, roll(value, 2 * j + 2), roll(value, 2 * j))
+        else:
+            value = roll(value, 2 * j + 1)
+        packs[p] = jnp.where(pair == j, value, packs[p])
+
+    def z_ends(i, x, t):
+        rows = slice(T * (t - 1), T * t)
+        return jnp.where(lane < HALF, pop[1, OPPOSITE[i], x, rows], pop[1, i, x, rows])
+
+    def pack_signs(x):
+        for t in range(1, YT + 1):
+            for k in range(2):
+                value = S[k, 2 + x, T * t:T * t + T]
+                put(0, k, 0, t, x, value)
+                put(0, k, 1, t, x, value, inside=True)
+            for d in range(3):
+                put(*V_PLACE[d], t, x, V[d, 1 + x, T * (t - 1):T * t])
+            if x in (0, X - 1):
+                out_i, in_i = (Z_UP[1], Z_UP[2]) if x else (Z_UP[2], Z_UP[1])
+                rows = slice(T * (t - 1), T * t)
+                value = jnp.where(lane < HALF, pop[1, OPPOSITE[in_i], x, rows], pop[1, out_i, x, rows])
+                put(1, 1, 1, t, x, value)
+
     loads[0].wait()
     for n in range(2):
         loads[1 + n].wait()
         for x in range(cuts[n], cuts[n + 1]):
             moments(x)
-
-    @pl.when(is_far)
-    def _():
-        pl.semaphore_wait(near_sem, 1)
-
-    first_up = lax.rem(me[0], 4) != 1
-    sides = [jnp.where(first_up, 1, -1), jnp.where(first_up, -1, 1)]
-
-    def send_x_signs(side):
-        up = side > 0
-        src = jnp.where(up, X, 2)
-        dst = jnp.where(up, 0, X + 2)
-        send("xS", S.at[:, pl.ds(src, 2), inner], S.at[:, pl.ds(dst, 2), inner],
-             (side, 0, 0), 4 * YT)
-
-    def send_x_bulk(side):
-        up = side > 0
-        n = jnp.where(up, 0, 1)
-        to = (side, 0, 0)
-        send("xB", V.at[:, jnp.where(up, X, 1), 0:Y], XB.at[n, 0:3], to, 3 * YT)
-        for m, i in enumerate(X_UP):
-            send("xB", pop.at[1, jnp.where(up, i, OPPOSITE[i]), jnp.where(up, X - 1, 0)],
-                 XB.at[n, 3 + m], to, YT)
-
-    send_x_signs(sides[0])
-    for n, side in enumerate((1, -1)):
-        tile = slice(Y - T, Y) if side > 0 else slice(0, T)
-        wide = slice(Y, Y + T) if side > 0 else slice(T, 2 * T)
-        to = (0, side, 0)
-        send("y", S.at[:, 2:2 + X, wide], YR.at[n, 0:2], to, 2 * X)
-        send("y", V.at[:, 1:1 + X, tile], YR.at[n, 2:5], to, 3 * X)
-        for m, i in enumerate(Y_UP):
-            i = i if side > 0 else OPPOSITE[i]
-            send("y", pop.at[1, i, :, tile], YR.at[n, 5 + m], to, X)
-
-    blank = jnp.zeros((T, LANES), jnp.float32)
-    packs = [blank, blank, blank, blank]
-    POP_PLACE = [(2, 0, 0), (2, 0, 1), (2, 1, 0), (2, 1, 1), (3, 1, 0)]
-    V_PLACE = [(1, 0, 0), (1, 0, 1), (1, 1, 0)]
-
-    def put(p, h, b, t, x, value):
-        j = (h * HALF + t * stride_t + (b * X + x) * 2) // 2
-        packs[p] = jnp.where(pair == j, roll(value, 2 * j + 1), packs[p])
-
-    for x in range(X):
-        for t in range(1, YT + 1):
-            rows = slice(T * t, T * t + T)
-            rows_v = slice(T * (t - 1), T * t)
-            for k in range(2):
-                value = S[k, 2 + x, rows]
-                put(0, k, 0, t, x, value)
-                put(0, k, 1, t, x, jnp.where(lane < HALF, roll(value, -1), roll(value, 1)))
-            for d in range(3):
-                put(*V_PLACE[d], t, x, V[d, 1 + x, rows_v])
-            for g, i in enumerate(Z_UP):
-                value = jnp.where(lane < HALF, pop[1, OPPOSITE[i], x, rows_v], pop[1, i, x, rows_v])
-                put(*POP_PLACE[g], t, x, value)
+        for x in range(cuts[n], cuts[n + 1]):
+            pack_signs(x)
+
     place = slot % X
-    diag = jnp.where((place == X - 1) == even, roll(packs[2], HALF), roll(packs[2], 2 * X))
-    packs[1] = jnp.where((half == 1) & (slot >= X) & (slot < 2 * X), diag, packs[1])
 
     def edges(v, q):
         return jnp.where(upper, roll(v, (q - 1) * stride_t), roll(v, (q - YT) * stride_t))
 
-    merged = edges(packs[0], 0)
-    for p in range(1, 4):
-        merged = jnp.where(tile_t == p, edges(packs[p], p), merged)
-    for p in range(4):
-        ZS[p] = packs[p]
-    ZS[4] = merged
     for n in range(2):
         if n == 0:
             tile = jnp.where(place >= X - 2, packs[0], roll(packs[1], -2 * (X - 1)))
@@ -296,31 +260,108 @@
             packed = jnp.where(at, roll_rows(fields[f], 2 * f), packed)
         XSND[n, 3] = packed
 
+    top_z = me[2] == count[2] - 1
+    not_top = jnp.logical_not(top_z)
+
+    def tell(sem):
+        pl.semaphore_signal(sem, inc=1, device_id=partner, device_id_type=MESH)
+
+    def learn_far():
+        pl.semaphore_wait(barrier, far_count)
+        tell(far_sem)
+
+    @pl.when(is_near)
+    def _():
+        pl.semaphore_wait(barrier, near_count)
+        tell(near_sem)
+
+    @pl.when(is_far & top_z)
+    def _():
+        learn_far()
+
+    @pl.when(is_far)
+    def _():
+        pl.semaphore_wait(near_sem, 1)
+
+    first_up = lax.rem(me[0], 4) != 1
+    sides = [jnp.where(first_up, 1, -1), jnp.where(first_up, -1, 1)]
+
+    def send_x_signs(side):
+        up = side > 0
+        src = jnp.where(up, X, 2)
+        dst = jnp.where(up, 0, X + 2)
+        send("xS", S.at[:, pl.ds(src, 2), inner], S.at[:, pl.ds(dst, 2), inner],
+             (side, 0, 0), 4 * YT)
+
+    def send_x_bulk(side):
+        up = side > 0
+        n = jnp.where(up, 0, 1)
+        to = (side, 0, 0)
+        send("xB", V.at[:, jnp.where(up, X, 1), 0:Y], XB.at[n, 0:3], to, 3 * YT)
+        for m, i in enumerate(X_UP):
+            send("xB", pop.at[1, jnp.where(up, i, OPPOSITE[i]), jnp.where(up, X - 1, 0)],
+                 XB.at[n, 3 + m], to, YT)
+
+    def send_diagonal():
+        for n, side in enumerate((1, -1)):
+            for m, dz in enumerate((1, -1)):
+                send("zD", XSND.at[n, 0], ZD.at[m, n, 0], (side, 0, dz), 1)
+                for sy in y_sides:
+                    send("zD", XSND.at[n, 0], ZD.at[m, n, 1 + y_slot[-sy]], (side, sy, dz), 1)
+
+    @pl.when(top_z)
+    def _():
+        @pl.when(is_near)
+        def _():
+            pl.semaphore_wait(far_sem, 1)
+
+        send_diagonal()
+
+    send_x_signs(sides[0])
     for n, side in enumerate((1, -1)):
         send("xE", XSND.at[n, 0:1], XE.at[n, 0:1], (side, 0, 0), 1)
         for sy in y_sides:
             m = 1 + 4 * y_slot[-sy]
             send("xE", XSND.at[n], XE.at[n, m:m + 4], (side, sy, 0), 4)
-    for sy in y_sides:
-        send("yW", ZS.at[4], YW.at[y_slot[-sy]], (0, sy, 0), 1)
+    for n, side in enumerate((1, -1)):
+        tile = slice(Y - T, Y) if side > 0 else slice(0, T)
+        wide = slice(Y, Y + T) if side > 0 else slice(T, 2 * T)
+        to = (0, side, 0)
+        send("y", S.at[:, 2:2 + X, wide], YR.at[n, 0:2], to, 2 * X)
+        send("y", V.at[:, 1:1 + X, tile], YR.at[n, 2:5], to, 3 * X)
+        for m, i in enumerate(Y_UP):
+            i = i if side > 0 else OPPOSITE[i]
+            send("y", pop.at[1, i, :, tile], YR.at[n, 5 + m], to, X)
     send_x_bulk(sides[0])
     send_x_signs(sides[1])
     send_x_bulk(sides[1])
 
-    @pl.when(is_far)
+    for x in range(X):
+        for t in range(1, YT + 1):
+            for g, i in enumerate(Z_UP):
+                put(*POP_PLACE[g], t, x, z_ends(i, x, t))
+    merged = edges(packs[0], 0)
+    for p in range(1, 4):
+        merged = jnp.where(tile_t == p, edges(packs[p], p), merged)
+    for p in range(4):
+        ZS[p] = packs[p]
+    ZS[4] = merged
+    for sy in y_sides:
+        send("yW", ZS.at[4], YW.at[y_slot[-sy]], (0, sy, 0), 1)
+
+    @pl.when(not_top)
     def _():
-        pl.semaphore_wait(barrier, far_count)
-        pl.semaphore_signal(far_sem, inc=1, device_id=partner, device_id_type=MESH)
-
-    @pl.when(is_near)
-    def _():
-        pl.semaphore_wait(far_sem, 1)
-
-    for n, side in enumerate((1, -1)):
-        for m, dz in enumerate((1, -1)):
-            send("zD", XSND.at[n, 0], ZD.at[m, n, 0], (side, 0, dz), 1)
-            for sy in y_sides:
-                send("zD", XSND.at[n, 0], ZD.at[m, n, 1 + y_slot[-sy]], (side, sy, dz), 1)
+        @pl.when(is_far)
+        def _():
+            learn_far()
+
+        @pl.when(is_near)
+        def _():
+            pl.semaphore_wait(far_sem, 1)
+
+        send_diagonal()
+
+    sent[0] -= 4 * (1 + NY)
     for m, dz in enumerate((1, -1)):
         send("zF", ZS.at[0:4], ZF.at[m, 0:4], (0, 0, dz), 4)
         for sy in y_sides:
@@ -480,13 +521,13 @@
     def x_down(v):
         return roll(v, 2)
 
-    def y_up(v):
+    def y_up(v, n=0):
         r = roll_rows(v, -1)
-        return jnp.where(row == T - 1, roll(r, -stride_t), r)
-
-    def y_down(v):
+        return jnp.where(row == T - 1, roll(r, n - stride_t), roll(r, n))
+
+    def y_down(v, n=0):
         r = roll_rows(v, 1)
-        return jnp.where(row == 0, roll(r, stride_t), r)
+        return jnp.where(row == 0, roll(r, n + stride_t), roll(r, n))
 
     def collide_z(s0, s1, s2, t1, t2, olds):
         other1, other2 = roll(t1, HALF), roll(t2, HALF)
@@ -505,12 +546,12 @@
         c2 = 2.0 * p2 + (xs[2] + ys[2])
         sign = jnp.where(even, 1.0, -1.0)
         grads = [
-            (x_up(a) - x_down(a)) * (1.0 / 36.0),
-            (y_up(b) - y_down(b)) * (1.0 / 36.0),
-            (c0 - c2) * (sign * (1.0 / 36.0)),
+            roll(a, HALF - 2) - roll(a, HALF + 2),
+            y_up(b, HALF) - y_down(b, HALF),
+            roll((c0 - c2) * sign, HALF),
         ]
-        factor = jnp.where(lower, COUPLING * RELAX[0], COUPLING * RELAX[1])
-        u = [common[d] - factor * roll(grads[d], HALF) for d in range(3)]
+        factor = jnp.where(lower, COUPLING * RELAX[0] / 36.0, COUPLING * RELAX[1] / 36.0)
+        u = [common[d] - factor * grads[d] for d in range(3)]
         rho = p1 * jnp.where(lower, INV[0], INV[1])
         keep = jnp.where(lower, KEEP[0], KEEP[1])
         flat = flat_of(u)
@@ -520,12 +561,11 @@
             old = jnp.where(beyond, t2, olds[g]) if c[0] else olds[g]
             value = one_way(rho * WEIGHTS[i], flat, along_of(i, u), sign)
             value = value + keep * jnp.where(lower, 0.0, old)
-            if c[0]:
-                value = jnp.where(even, roll(value, 2 * c[0]), roll(value, -2 * c[0]))
             if c[1]:
                 a, b = (y_down, y_up) if c[1] > 0 else (y_up, y_down)
-                value = jnp.where(even, a(value), b(value))
-            value = swap(value)
+                value = jnp.where(even, b(value, -1), a(value, 1))
+            else:
+                value = jnp.where(even, roll(value, -1 - 2 * c[0]), roll(value, 1 + 2 * c[0]))
             for k in range(2):
                 for x in range(X):
                     for t in range(1, YT + 1):
@@ -551,35 +591,6 @@
     for x in range(X):
         prepare(2 + x)
 
-    def with_rows(tile, w_low, w_high):
-        return jnp.where(own_t, tile, jnp.where(tile_t == 0, w_low, w_high))
-
-    def by_row(low_part, high_part):
-        return low_part if NY == 1 else ends(low_part, high_part)
-
-    top = stride_t * (YT + 1)
-
-    await_("zF", ZF)
-    faces = [jnp.where(even, ZF[0, p], ZF[1, p]) for p in range(4 + NY)]
-    z_rows = by_row(faces[4 + y_slot[1]], faces[4 + y_slot[-1]])
-    full = [
-        with_rows(faces[p], roll(z_rows, -stride_t * p), roll(z_rows, top - stride_t * p))
-        for p in range(4)
-    ]
-    center = [[roll(full[p], 2 * (2 - b * X)) for b in range(2)] for p in range(2)]
-    olds = []
-    for p, h, b in POP_PLACE:
-        olds.append(roll(full[p], 2 * (2 - b * X) + HALF * (1 - h)))
-    near_signs = swap(center[0][0])
-    for x in range(X):
-        complete(2 + x, near_signs)
-    for x in range(X):
-        sums(2 + x)
-    for x in range(1, X - 1):
-        collide_own(x)
-        collide_rows(x)
-
-    await_("yW", YW)
     await_("xS", S.at[:, 0:4, inner])
     await_("xE", XE)
     for n in range(2):
@@ -604,6 +615,14 @@
     for p in outer:
         prepare(p)
 
+    def with_rows(tile, w_low, w_high):
+        return jnp.where(own_t, tile, jnp.where(tile_t == 0, w_low, w_high))
+
+    def by_row(low_part, high_part):
+        return low_part if NY == 1 else ends(low_part, high_part)
+
+    top = stride_t * (YT + 1)
+
     def assemble(middle, left, right, shift_left, shift_right):
         return jnp.where(
             slot < 2,
@@ -611,6 +630,7 @@
             jnp.where(slot >= X + 2, roll(right, 2 * shift_right), middle),
         )
 
+    await_("yW", YW)
     y_rows = by_row(YW[y_slot[1]], YW[y_slot[-1]])
     own = with_rows(ZS[0], y_rows, roll(y_rows, top))
     beside = []
@@ -618,6 +638,26 @@
         w = by_row(XE[n, 1 + 4 * y_slot[1]], XE[n, 1 + 4 * y_slot[-1]])
         beside.append(with_rows(XE[n, 0], w, roll(w, top)))
     s0 = swap(assemble(roll(own, 4), beside[0], beside[1], 2 - X, X + 2))
+
+    await_("zF", ZF)
+    faces = [jnp.where(even, ZF[0, p], ZF[1, p]) for p in range(4 + NY)]
+    z_rows = by_row(faces[4 + y_slot[1]], faces[4 + y_slot[-1]])
+    full = [
+        with_rows(faces[p], roll(z_rows, -stride_t * p), roll(z_rows, top - stride_t * p))
+        for p in range(4)
+    ]
+    center = [[roll(full[p], 2 * (2 - b * X)) for b in range(2)] for p in range(2)]
+    olds = []
+    for p, h, b in POP_PLACE:
+        olds.append(roll(full[p], 2 * (2 - b * X) + HALF * (1 - h)))
+    near_signs = swap(center[0][0])
+    for x in range(X):
+        complete(2 + x, near_signs)
+    for x in range(X):
+        sums(2 + x)
+    for x in range(1, X - 1):
+        collide_own(x)
+        collide_rows(x)
 
     await_("zD", ZD)
     diags = []

time: 13.8 us -> 13 us (0.942)
  Pallas kernels: 12.7 us -> 11.8 us
    pallas_call x1, Pallas kernels: 12.7 us -> 11.8 us  [body(): pl.pallas_call(step_kernel, out_shape=pltpu.VMEM(populations.shape, f32),...]
where the time goes in v3:
time: 13 us; the launch traced here: 12.8 us
  Pallas kernels  11.8 us (91%)
  local copies, waits for them, and re-layouts  1.04 us (8%)
    pallas_call x1, Pallas kernels, body(): pl.pallas_call(step_kernel, out_shape=pltpu.VMEM(populations.shape, f32),...  11.8 us
    unnamed x1, local copies, waits for them, and re-layouts  1.04 us

profile of v3, /device:TPU:0, one launch (start us, length us, event | category | flops | bytes accessed | tf_op | source)
XLA Modules:
  0.0 12.8 jit_solution(4536801829175285996)
XLA Ops:
  0.0 11.8 %shard_map.28 = f32[2,19,4,16,128]{4,3,2,1,0:T(8,128)S(1)} custom-call(f32[2,19,4,16,128]{4,3,2,1,0:T(8,128)} %pop_hbm.1, s32[4,16,128]{2,1,0:T(8,128)} %solid_hbm.1), custom_call_target="tpu_custom_call" | custom-call | tf_op jit(solution)/shard_map/pallas_call | solution.py:707
  11.8 1.0 %copy.4 = f32[2,19,4,16,128]{4,3,2,1,0:T(8,128)} copy(f32[2,19,4,16,128]{4,3,2,1,0:T(8,128)S(1)} %shard_map.28) | data formatting | bytes 2490368

commit v4 on v3

--- a/solution.py
+++ b/solution.py
@@ -270,19 +270,6 @@
         pl.semaphore_wait(barrier, far_count)
         tell(far_sem)
 
-    @pl.when(is_near)
-    def _():
-        pl.semaphore_wait(barrier, near_count)
-        tell(near_sem)
-
-    @pl.when(is_far & top_z)
-    def _():
-        learn_far()
-
-    @pl.when(is_far)
-    def _():
-        pl.semaphore_wait(near_sem, 1)
-
     first_up = lax.rem(me[0], 4) != 1
     sides = [jnp.where(first_up, 1, -1), jnp.where(first_up, -1, 1)]
 
@@ -309,15 +296,58 @@
                 for sy in y_sides:
                     send("zD", XSND.at[n, 0], ZD.at[m, n, 1 + y_slot[-sy]], (side, sy, dz), 1)
 
+    ZS[5] = packs[0]
+
+    def pack_faces():
+        for x in range(X):
+            for t in range(1, YT + 1):
+                for g, i in enumerate(Z_UP):
+                    put(*POP_PLACE[g], t, x, z_ends(i, x, t))
+        merged = edges(packs[0], 0)
+        for p in range(1, 4):
+            merged = jnp.where(tile_t == p, edges(packs[p], p), merged)
+        for m in range(2):
+            one, two = packs[2 * m], packs[2 * m + 1]
+            ZS[m] = jnp.where(even, one, roll(two, 1))
+            ZS[2 + m] = jnp.where(even, roll(two, -1), one)
+        ZS[4] = merged
+        packs[2] = packs[3] = blank
+
+    def send_faces():
+        for m, dz in enumerate((1, -1)):
+            send("zF", ZS.at[2 * m:2 * m + 2], ZF.at[m, 0:2], (0, 0, dz), 2)
+            for sy in y_sides:
+                send("zF", ZS.at[4], ZF.at[m, 2 + y_slot[-sy]], (0, sy, dz), 1)
+
+    @pl.when(is_far & top_z)
+    def _():
+        learn_far()
+
+    @pl.when(is_near & top_z)
+    def _():
+        pl.semaphore_wait(far_sem, 1)
+
+    counted = sent[0]
+
     @pl.when(top_z)
     def _():
-        @pl.when(is_near)
-        def _():
-            pl.semaphore_wait(far_sem, 1)
-
         send_diagonal()
+        pack_faces()
+        send_faces()
+
+    sent[0] = counted
+
+    @pl.when(is_near)
+    def _():
+        pl.semaphore_wait(barrier, near_count)
+        tell(near_sem)
+
+    @pl.when(is_far)
+    def _():
+        pl.semaphore_wait(near_sem, 1)
 
     send_x_signs(sides[0])
+    send_x_signs(sides[1])
     for n, side in enumerate((1, -1)):
         send("xE", XSND.at[n, 0:1], XE.at[n, 0:1], (side, 0, 0), 1)
         for sy in y_sides:
@@ -333,39 +363,27 @@
             i = i if side > 0 else OPPOSITE[i]
             send("y", pop.at[1, i, :, tile], YR.at[n, 5 + m], to, X)
     send_x_bulk(sides[0])
-    send_x_signs(sides[1])
     send_x_bulk(sides[1])
 
-    for x in range(X):
-        for t in range(1, YT + 1):
-            for g, i in enumerate(Z_UP):
-                put(*POP_PLACE[g], t, x, z_ends(i, x, t))
-    merged = edges(packs[0], 0)
-    for p in range(1, 4):
-        merged = jnp.where(tile_t == p, edges(packs[p], p), merged)
-    for p in range(4):
-        ZS[p] = packs[p]
-    ZS[4] = merged
+    @pl.when(not_top)
+    def _():
+        pack_faces()
+
     for sy in y_sides:
         send("yW", ZS.at[4], YW.at[y_slot[-sy]], (0, sy, 0), 1)
 
+    @pl.when(is_far & not_top)
+    def _():
+        learn_far()
+
+    @pl.when(is_near & not_top)
+    def _():
+        pl.semaphore_wait(far_sem, 1)
+
     @pl.when(not_top)
     def _():
-        @pl.when(is_far)
-        def _():
-            learn_far()
-
-        @pl.when(is_near)
-        def _():
-            pl.semaphore_wait(far_sem, 1)
-
         send_diagonal()
-
-    sent[0] -= 4 * (1 + NY)
-    for m, dz in enumerate((1, -1)):
-        send("zF", ZS.at[0:4], ZF.at[m, 0:4], (0, 0, dz), 4)
-        for sy in y_sides:
-            send("zF", ZS.at[4], ZF.at[m, 4 + y_slot[-sy]], (0, sy, dz), 1)
+        send_faces()
 
     await_("y", YR)
     for x in range(X):
@@ -397,11 +415,11 @@
     def spread(tile, k, t, xx):
         return roll(tile, LANES - 1 - (k * HALF + t * stride_t + 2 * xx))
 
-    def complete(p, signs):
+    def complete(p, signs, at):
         for k in range(2):
             for t in range(YT + 1):
                 rows = slice(T * t, T * t + T)
-                edge = spread(signs, k, t, p)
+                edge = spread(signs, k, t, at)
                 above = jnp.where(last, edge, SU[k, p, rows])
                 below = jnp.where(first, edge, SD[k, p, rows])
                 size = jnp.abs(S[k, p, rows])
@@ -632,7 +650,7 @@
 
     await_("yW", YW)
     y_rows = by_row(YW[y_slot[1]], YW[y_slot[-1]])
-    own = with_rows(ZS[0], y_rows, roll(y_rows, top))
+    own = with_rows(ZS[5], y_rows, roll(y_rows, top))
     beside = []
     for n in range(2):
         w = by_row(XE[n, 1 + 4 * y_slot[1]], XE[n, 1 + 4 * y_slot[-1]])
@@ -640,8 +658,16 @@
     s0 = swap(assemble(roll(own, 4), beside[0], beside[1], 2 - X, X + 2))
 
     await_("zF", ZF)
-    faces = [jnp.where(even, ZF[0, p], ZF[1, p]) for p in range(4 + NY)]
-    z_rows = by_row(faces[4 + y_slot[1]], faces[4 + y_slot[-1]])
+    one, two = ZF[0, 0], ZF[1, 0]
+    rows_z = [jnp.where(even, ZF[0, 2 + m], ZF[1, 2 + m]) for m in range(NY)]
+    z_rows = by_row(rows_z[y_slot[1]], rows_z[y_slot[-1]])
+    near_signs = jnp.where(even, roll(two, -1), roll(one, 1))
+    near_signs = jnp.where(tile_t == 0, swap(z_rows), near_signs)
+    faces = []
+    for m in range(2):
+        one, two = ZF[0, m], ZF[1, m]
+        faces.append(jnp.where(even, one, two))
+        faces.append(jnp.where(even, roll(one, -1), roll(two, 1)))
     full = [
         with_rows(faces[p], roll(z_rows, -stride_t * p), roll(z_rows, top - stride_t * p))
         for p in range(4)
@@ -650,9 +676,8 @@
     olds = []
     for p, h, b in POP_PLACE:
         olds.append(roll(full[p], 2 * (2 - b * X) + HALF * (1 - h)))
-    near_signs = swap(center[0][0])
     for x in range(X):
-        complete(2 + x, near_signs)
+        complete(2 + x, near_signs, x)
     for x in range(X):
         sums(2 + x)
     for x in range(1, X - 1):
@@ -660,18 +685,19 @@
         collide_rows(x)
 
     await_("zD", ZD)
-    diags = []
+    diags, far_signs = [], []
     for n in range(2):
         merged = [jnp.where(even, ZD[0, n, q], ZD[1, n, q]) for q in range(1 + NY)]
         w = by_row(merged[1 + y_slot[1]], merged[1 + y_slot[-1]])
+        far_signs.append(swap(jnp.where(tile_t == 0, w, merged[0])))
         diags.append(with_rows(merged[0], w, roll(w, top)))
+    for m in range(2):
+        complete(m, far_signs[0], X - 2 + m)
+        complete(X + 2 + m, far_signs[1], m)
     s1, s2 = [
         assemble(center[0][b], *diags, -(b * X + X - 2), X + 2 - b * X) for b in range(2)
     ]
     t1, t2 = [assemble(center[1][b], *diags, 1 - b * X, 3 - b * X) for b in range(2)]
-    signs = swap(s1)
-    for p in outer:
-        complete(p, signs)
     for p in outer:
         sums(p)
     for x in (0, X - 1):
@@ -699,7 +725,7 @@
     XX = X + 4
     NY = 1 if lax.axis_size("gy") == 2 else 2
     YT = Y // T
-    tiles = 20 * X + 24 * YT + 14 + 15 * NY
+    tiles = 20 * X + 24 * YT + 10 + 15 * NY
 
     def vmem(*shape):
         return pltpu.VMEM(shape, f32)
@@ -728,9 +754,9 @@
             vmem(2, T, Z),
             vmem(2, 4, T, LANES),
             vmem(2, 1 + 4 * NY, T, LANES),
-            vmem(5, T, LANES),
+            vmem(6, T, LANES),
             vmem(NY, T, LANES),
-            vmem(2, 4 + NY, T, LANES),
+            vmem(2, 2 + NY, T, LANES),
             vmem(2, 2, 1 + NY, T, LANES),
             vmem(tiles, T, LANES),
             dma((3,)),

time: 13 us -> 12.9 us (level)
  no operation moved by 1% of the time
where the time goes in v4:
time: 12.9 us; the launch traced here: 12.8 us
  Pallas kernels  11.8 us (91%)
  local copies, waits for them, and re-layouts  1.04 us (8%)
    pallas_call x1, Pallas kernels, body(): pl.pallas_call(step_kernel, out_shape=pltpu.VMEM(populations.shape, f32),...  11.8 us
    unnamed x1, local copies, waits for them, and re-layouts  1.04 us

profile of v4, /device:TPU:0, one launch (start us, length us, event | category | flops | bytes accessed | tf_op | source)
XLA Modules:
  0.0 12.8 jit_solution(3399011458887852867)
XLA Ops:
  0.0 11.8 %shard_map.28 = f32[2,19,4,16,128]{4,3,2,1,0:T(8,128)S(1)} custom-call(f32[2,19,4,16,128]{4,3,2,1,0:T(8,128)} %pop_hbm.1, s32[4,16,128]{2,1,0:T(8,128)} %solid_hbm.1), custom_call_target="tpu_custom_call" | custom-call | tf_op jit(solution)/shard_map/pallas_call | solution.py:733
  11.8 1.0 %copy.4 = f32[2,19,4,16,128]{4,3,2,1,0:T(8,128)} copy(f32[2,19,4,16,128]{4,3,2,1,0:T(8,128)S(1)} %shard_map.28) | data formatting | bytes 2490368

commit v5 on v4

--- a/solution.py
+++ b/solution.py
@@ -62,7 +62,7 @@
 
 
 def step_kernel(pop_hbm, solid_hbm, out, pop, solid, S, SU, SD, psi, H, O, A, V, post, zpost,
-                YR, WP, XB, XWP, XSND, XE, ZS, YW, ZF, ZD, tally, load_sem, send_sem, recv_sem,
+                YR, WP, XB, XWP, XSND, XE, ZS, YX, ZF, ZD, tally, load_sem, send_sem, recv_sem,
                 near_sem, far_sem):
     X, Y, Z = solid.shape
     YT = Y // T
@@ -146,7 +146,7 @@
     def swap(v):
         return jnp.where(even, roll(v, -1), roll(v, 1))
 
-    GROUPS = {"y": 0, "yW": 1, "xS": 2, "xE": 3, "zF": 4, "zD": 5, "xB": 6}
+    GROUPS = {"y": 0, "yX": 1, "xS": 2, "xE": 3, "zF": 4, "zD": 5, "xB": 6}
     sent = [0]
 
     def send(group, src, dst, offset, tiles):
@@ -243,13 +243,7 @@
         return jnp.where(upper, a, b)
 
     t_first, t_last = slice(0, T), slice(Y - T, Y)
-    s_first, s_last = slice(T, 2 * T), slice(Y, Y + T)
-    keep_rows = (row < 2) | (row >= T - 2)
     for n, side in enumerate((1, -1)):
-        planes = (X, X + 1) if side > 0 else (2, 3)
-        for m, p in enumerate(planes):
-            both = [ends(S[k, p, s_first], S[k, p, s_last]) for k in range(2)]
-            XSND[n, 1 + m] = jnp.where(keep_rows, both[0], roll_rows(both[1], 4))
         x = X - 1 if side > 0 else 0
         up, down = INDEX[(side, 1, 0)], INDEX[(side, -1, 0)]
         fields = [ends(V[d, 1 + x, t_first], V[d, 1 + x, t_last]) for d in range(3)]
@@ -258,7 +252,7 @@
         for f in range(1, 4):
             at = (row == 2 * f - 1) | (row == 2 * f)
             packed = jnp.where(at, roll_rows(fields[f], 2 * f), packed)
-        XSND[n, 3] = packed
+        XSND[n, 1] = packed
 
     top_z = me[2] == count[2] - 1
     not_top = jnp.logical_not(top_z)
@@ -349,10 +343,8 @@
     send_x_signs(sides[0])
     send_x_signs(sides[1])
     for n, side in enumerate((1, -1)):
-        send("xE", XSND.at[n, 0:1], XE.at[n, 0:1], (side, 0, 0), 1)
         for sy in y_sides:
-            m = 1 + 4 * y_slot[-sy]
-            send("xE", XSND.at[n], XE.at[n, m:m + 4], (side, sy, 0), 4)
+            send("xE", XSND.at[n, 1], XE.at[n, y_slot[-sy]], (side, sy, 0), 1)
     for n, side in enumerate((1, -1)):
         tile = slice(Y - T, Y) if side > 0 else slice(0, T)
         wide = slice(Y, Y + T) if side > 0 else slice(T, 2 * T)
@@ -363,14 +355,10 @@
             i = i if side > 0 else OPPOSITE[i]
             send("y", pop.at[1, i, :, tile], YR.at[n, 5 + m], to, X)
     send_x_bulk(sides[0])
-    send_x_bulk(sides[1])
 
     @pl.when(not_top)
     def _():
         pack_faces()
-
-    for sy in y_sides:
-        send("yW", ZS.at[4], YW.at[y_slot[-sy]], (0, sy, 0), 1)
 
     @pl.when(is_far & not_top)
     def _():
@@ -385,6 +373,7 @@
         send_diagonal()
         send_faces()
 
+    send_x_bulk(sides[1])
     await_("y", YR)
     for x in range(X):
         for k in range(2):
@@ -610,25 +599,26 @@
         prepare(2 + x)
 
     await_("xS", S.at[:, 0:4, inner])
+    for n, side in enumerate((1, -1)):
+        wide = slice(Y, Y + T) if side > 0 else slice(T, 2 * T)
+        for m, p in enumerate((0, X + 2)):
+            send("yX", S.at[:, p:p + 2, wide], YX.at[n, m], (0, side, 0), 4)
     await_("xE", XE)
     for n in range(2):
-        planes = (0, 1) if n == 0 else (X + 2, X + 3)
-        ups, downs = 1 + 4 * y_slot[1], 1 + 4 * y_slot[-1]
-        for m, p in enumerate(planes):
-            value = XE[n, ups + 1 + m]
-            if NY > 1:
-                value = jnp.where(row % 4 < 2, value, XE[n, downs + 1 + m])
-            other = roll_rows(value, 4)
-            for k, w in ((0, value), (1, other)):
-                S[k, p, low] = w
-                S[k, p, high] = w
-        value = XE[n, ups + 3]
+        value = XE[n, y_slot[1]]
         if NY > 1:
-            value = jnp.where(row % 2 == 0, value, XE[n, downs + 3])
+            value = jnp.where(row % 2 == 0, value, XE[n, y_slot[-1]])
         plane = 0 if n == 0 else X + 1
         for d in range(3):
             V[d, plane, Y:Y + T] = roll_rows(value, -2 * d)
         XWP[n] = roll_rows(value, -6)
+    await_("yX", YX)
+    for m, base in enumerate((0, X + 2)):
+        for q in range(2):
+            for k in range(2):
+                value = ends(YX[1, m, k, q], YX[0, m, k, q])
+                S[k, base + q, low] = value
+                S[k, base + q, high] = value
     outer = [0, 1, X + 2, X + 3]
     for p in outer:
         prepare(p)
@@ -648,14 +638,13 @@
             jnp.where(slot >= X + 2, roll(right, 2 * shift_right), middle),
         )
 
-    await_("yW", YW)
-    y_rows = by_row(YW[y_slot[1]], YW[y_slot[-1]])
-    own = with_rows(ZS[5], y_rows, roll(y_rows, top))
-    beside = []
-    for n in range(2):
-        w = by_row(XE[n, 1 + 4 * y_slot[1]], XE[n, 1 + 4 * y_slot[-1]])
-        beside.append(with_rows(XE[n, 0], w, roll(w, top)))
-    s0 = swap(assemble(roll(own, 4), beside[0], beside[1], 2 - X, X + 2))
+    s0 = roll(ZS[5], 4)
+    for p in range(XX):
+        for k in range(2):
+            for t in ([0] if 2 <= p < X + 2 else range(YT + 1)):
+                j = (k * HALF + t * stride_t) // 2 + p
+                s0 = jnp.where(pair == j, roll(S[k, p, T * t:T * t + T], 2 * j + 1), s0)
+    s0 = swap(jnp.where(tile_t == YT + 1, roll(s0, top), s0))
 
     await_("zF", ZF)
     one, two = ZF[0, 0], ZF[1, 0]
@@ -725,7 +714,7 @@
     XX = X + 4
     NY = 1 if lax.axis_size("gy") == 2 else 2
     YT = Y // T
-    tiles = 20 * X + 24 * YT + 10 + 15 * NY
+    tiles = 20 * X + 24 * YT + 24 + 8 * NY
 
     def vmem(*shape):
         return pltpu.VMEM(shape, f32)
@@ -752,10 +741,10 @@
             vmem(5, X, T, Z),
             vmem(2, 8, Y, Z),
             vmem(2, T, Z),
-            vmem(2, 4, T, LANES),
-            vmem(2, 1 + 4 * NY, T, LANES),
+            vmem(2, 2, T, LANES),
+            vmem(2, NY, T, LANES),
             vmem(6, T, LANES),
-            vmem(NY, T, LANES),
+            vmem(2, 2, 2, 2, T, LANES),
             vmem(2, 2 + NY, T, LANES),
             vmem(2, 2, 1 + NY, T, LANES),
             vmem(tiles, T, LANES),

time: 12.9 us -> 12.5 us (0.969)
  Pallas kernels: 11.8 us -> 11.3 us
    pallas_call x1, Pallas kernels: 11.8 us -> 11.3 us  [body(): pl.pallas_call(step_kernel, out_shape=pltpu.VMEM(populations.shape, f32),...]
where the time goes in v5:
time: 12.5 us; the launch traced here: 12.4 us
  Pallas kernels  11.3 us (90%)
  local copies, waits for them, and re-layouts  1.04 us (8%)
    pallas_call x1, Pallas kernels, body(): pl.pallas_call(step_kernel, out_shape=pltpu.VMEM(populations.shape, f32),...  11.3 us
    unnamed x1, local copies, waits for them, and re-layouts  1.04 us

profile of v5, /device:TPU:0, one launch (start us, length us, event | category | flops | bytes accessed | tf_op | source)
XLA Modules:
  0.0 12.4 jit_solution(2599496076762023643)
XLA Ops:
  0.0 11.3 %shard_map.28 = f32[2,19,4,16,128]{4,3,2,1,0:T(8,128)S(1)} custom-call(f32[2,19,4,16,128]{4,3,2,1,0:T(8,128)} %pop_hbm.1, s32[4,16,128]{2,1,0:T(8,128)} %solid_hbm.1), custom_call_target="tpu_custom_call" | custom-call | tf_op jit(solution)/shard_map/pallas_call | solution.py:722
  11.3 1.0 %copy.4 = f32[2,19,4,16,128]{4,3,2,1,0:T(8,128)} copy(f32[2,19,4,16,128]{4,3,2,1,0:T(8,128)S(1)} %shard_map.28) | data formatting | bytes 2490368

commit v6 on v5

--- a/solution.py
+++ b/solution.py
@@ -61,7 +61,39 @@
     return total
 
 
-def step_kernel(pop_hbm, solid_hbm, out, pop, solid, S, SU, SD, psi, H, O, A, V, post, zpost,
+def stream(x, out_at, refs, dirs=range(19)):
+    pop, solid, post, zpost, signs, out = refs
+    X, Y, Z = solid.shape
+    lane = lax.broadcasted_iota(jnp.int32, (Y, Z), 1)
+    first, last = lane == 0, lane == Z - 1
+    fluid = solid[x] == 0
+    for k in range(2):
+        for i in dirs:
+            c = VELOCITIES[i]
+            rows = slice(T - c[1], T - c[1] + Y)
+            read = post[k, i, 1 + x - c[0], rows]
+            if i:
+                if c[2]:
+                    shifted = pltpu.roll(read, c[2] % Z, 1)
+                    read = jnp.where(first if c[2] > 0 else last, zpost[k, Z_PAIR[i], x], shifted)
+                bounced = post[k, OPPOSITE[i], 1 + x, T:T + Y]
+                read = jnp.where(signs[c[2] % 3, 2 + x - c[0], rows] > 0.0, read, bounced)
+            out[k, i, out_at] = jnp.where(fluid, read, pop[k, i, x])
+
+
+def finish_kernel(pop, solid, post, zpost, signs, inside, out, ends, sem):
+    X, Y, Z = solid.shape
+    copies = [pltpu.make_async_copy(inside, out.at[:, :, 1:X - 1], sem.at[0])]
+    copies[0].start()
+    for n, x in enumerate((0, X - 1)):
+        stream(x, n, (pop, solid, post, zpost, signs, ends))
+        copies.append(pltpu.make_async_copy(ends.at[:, :, n], out.at[:, :, x], sem.at[1 + n]))
+        copies[-1].start()
+    for copy in copies:
+        copy.wait()
+
+
+def step_kernel(pop_hbm, solid_hbm, pop, solid, post, zpost, signs, inside, S, SU, SD, psi, H, O, A, V,
                 YR, WP, XB, XWP, XSND, XE, ZS, YX, ZF, ZD, tally, load_sem, send_sem, recv_sem,
                 near_sem, far_sem):
     X, Y, Z = solid.shape
@@ -404,11 +436,11 @@
     def spread(tile, k, t, xx):
         return roll(tile, LANES - 1 - (k * HALF + t * stride_t + 2 * xx))
 
-    def complete(p, signs, at):
+    def complete(p, columns, at):
         for k in range(2):
             for t in range(YT + 1):
                 rows = slice(T * t, T * t + T)
-                edge = spread(signs, k, t, at)
+                edge = spread(columns, k, t, at)
                 above = jnp.where(last, edge, SU[k, p, rows])
                 below = jnp.where(first, edge, SD[k, p, rows])
                 size = jnp.abs(S[k, p, rows])
@@ -418,8 +450,9 @@
                     H[k, p, r] = 2.0 * size + (a_above + a_below)
                     O[k, p, r] = a_above - a_below
                     if k == 0:
-                        SU[k, p, r] = above
-                        SD[k, p, r] = below
+                        signs[0, p, r] = S[k, p, rows]
+                        signs[2, p, r] = above
+                        signs[1, p, r] = below
 
     def sums(p):
         for k in range(2):
@@ -578,23 +611,6 @@
                     for t in range(1, YT + 1):
                         zpost[k, g, x, T * (t - 1):T * t] = spread(value, k, t, x + 2)
 
-    def stream(x):
-        fluid = solid[x] == 0
-        for k in range(2):
-            for i in range(19):
-                c = VELOCITIES[i]
-                rows = slice(T - c[1], T - c[1] + Y)
-                read = post[k, i, 1 + x - c[0], rows]
-                if i:
-                    if c[2]:
-                        at = first_y if c[2] > 0 else last_y
-                        read = jnp.where(at, zpost[k, Z_PAIR[i], x], roll(read, c[2]))
-                    p = 2 + x - c[0]
-                    signs = SD if c[2] > 0 else (SU if c[2] else S)
-                    bounced = post[k, OPPOSITE[i], 1 + x, inner]
-                    read = jnp.where(signs[0, p, rows] > 0.0, read, bounced)
-                out[k, i, x] = jnp.where(fluid, read, pop[k, i, x])
-
     for x in range(X):
         prepare(2 + x)
 
@@ -696,12 +712,10 @@
     for n in range(2):
         collide_corner(n)
     for x in range(1, X - 1):
-        stream(x)
+        stream(x, x - 1, (pop, solid, post, zpost, signs, inside))
     await_("xB", XB)
     for n in range(2):
         collide_plane(n)
-    for x in (0, X - 1):
-        stream(x)
     assert sent[0] == tally.shape[0]
     pltpu.make_async_copy(tally, tally, send_sem).wait()
 
@@ -719,14 +733,22 @@
     def vmem(*shape):
         return pltpu.VMEM(shape, f32)
 
-    return pl.pallas_call(
+    shapes = [
+        populations.shape,
+        solid.shape,
+        (2, 19, X + 2, R, Z),
+        (2, 5, X, Y, Z),
+        (3, XX, R, Z),
+        (2, 19, X - 2, Y, Z),
+    ]
+    types = [solid.dtype if n == 1 else f32 for n in range(6)]
+    in_vmem = pl.BlockSpec(memory_space=pltpu.VMEM)
+    state = pl.pallas_call(
         step_kernel,
-        out_shape=pltpu.VMEM(populations.shape, f32),
-        in_specs=[pl.BlockSpec(memory_space=pl.ANY)] * 2,
-        out_specs=pl.BlockSpec(memory_space=pltpu.VMEM),
+        out_shape=[pltpu.VMEM(a, b) for a, b in zip(shapes, types)],
+        in_specs=[pl.BlockSpec(memory_space=pltpu.HBM)] * 2,
+        out_specs=[in_vmem] * 6,
         scratch_shapes=[
-            vmem(*populations.shape),
-            pltpu.VMEM(solid.shape, jnp.int32),
             vmem(2, XX, R, Z),
             vmem(2, XX, R, Z),
             vmem(2, XX, R, Z),
@@ -735,8 +757,6 @@
             vmem(2, XX, R, Z),
             vmem(2, XX, Y + T, Z),
             vmem(3, X + 2, Y + T, Z),
-            vmem(2, 19, X + 2, R, Z),
-            vmem(2, 5, X, Y, Z),
             vmem(2, 10, X, T, Z),
             vmem(5, X, T, Z),
             vmem(2, 8, Y, Z),
@@ -754,8 +774,18 @@
             pltpu.SemaphoreType.REGULAR,
             pltpu.SemaphoreType.REGULAR,
         ],
-        compiler_params=pltpu.CompilerParams(collective_id=0, has_side_effects=True),
-    )(populations, solid)
+        compiler_params=pltpu.CompilerParams(
+            collective_id=0, has_side_effects=True, vmem_limit_bytes=24 * 2**20
+        ),
+    )(*[pltpu.with_memory_space_constraint(v, pltpu.HBM) for v in (populations, solid)])
+    return pl.pallas_call(
+        finish_kernel,
+        out_shape=jax.ShapeDtypeStruct(populations.shape, f32),
+        in_specs=[in_vmem] * 6,
+        out_specs=pl.BlockSpec(memory_space=pl.ANY),
+        scratch_shapes=[vmem(2, 19, 2, Y, Z), dma((3,))],
+        compiler_params=pltpu.CompilerParams(vmem_limit_bytes=16 * 2**20),
+    )(*state)
 
 
 def solution(mesh):

time: 12.5 us -> 12.4 us (level)
  local copies, waits for them, and re-layouts: 1.04 us -> 0 us
  Pallas kernels: 11.3 us -> 12.3 us
    unnamed x1 -> x0, local copies, waits for them, and re-layouts: 1.04 us -> none
    pallas_call x1 -> x2, Pallas kernels: 11.3 us -> 12.3 us  [the longest x1 11.2 us: body(): pl.pallas_call(step_kernel, out_shape=[pltpu.VMEM(a, b) for a, b in zip(s...]
where the time goes in v6:
time: 12.4 us; the launch traced here: 12.3 us
  Pallas kernels  12.3 us (99%)
    pallas_call x1, Pallas kernels, body(): pl.pallas_call(step_kernel, out_shape=[pltpu.VMEM(a, b) for a, b in zip(s...  11.2 us
    pallas_call x1, Pallas kernels, body(): pl.pallas_call(finish_kernel, out_shape=jax.ShapeDtypeStruct(populations....  1.07 us

profile of v6, /device:TPU:0, one launch (start us, length us, event | category | flops | bytes accessed | tf_op | source)
XLA Modules:
  0.0 12.3 jit_solution(1255088958786063066)
XLA Ops:
  0.0 11.2 %shard_map.28 = (f32[2,19,4,16,128]{4,3,2,1,0:T(8,128)S(1)}, s32[4,16,128]{2,1,0:T(8,128)S(1)}, f32[2,19,6,32,128]{4,3,2,1,0:T(8,128)S(1)}, f32[2,5,4,16,128]{4,...) custom-call(f32[2,19,4,16,128]{4,3,2,1,0:T(8,128)} %pop_hbm.1, ...), custom_call_target="tpu_custom_call" | custom-call | tf_op jit(solution)/shard_map/pallas_call | solution.py:746
  11.2 1.1 %shard_map.29 = f32[2,19,4,16,128]{4,3,2,1,0:T(8,128)} custom-call(f32[2,19,4,16,128]{4,3,2,1,0:T(8,128)S(1)} %get-tuple-element.11.pop, s32[4,16,128]{2,1,0:T(8,128)S(1)} %get-tuple-element.12.solid, f32[2,19,6,32,128]{4,3,2,1,0:T(8,128)S(1)} %get-tuple-element.13.post, f32[2,5,4,16,128]{4,3,2,1,0:T(8,128)S(1)} %get-tuple-element.14.zpost, ...), custom_call_target="tpu_custom_call" | custom-call | tf_op jit(solution)/shard_map/pallas_call | solution.py:781

commit v7 on v6

--- a/solution.py
+++ b/solution.py
@@ -61,6 +61,10 @@
     return total
 
 
+def reach(x, X):
+    return [i for i, c in enumerate(VELOCITIES) if 1 <= x - c[0] <= X - 2 and c[2] == 0]
+
+
 def stream(x, out_at, refs, dirs=range(19)):
     pop, solid, post, zpost, signs, out = refs
     X, Y, Z = solid.shape
@@ -113,9 +117,8 @@
     y_slot = {1: 0, -1: NY - 1}
 
     loads = [pltpu.make_async_copy(solid_hbm, solid, load_sem.at[0])]
-    cuts = [0, X // 2, X]
-    for n in range(2):
-        part = slice(cuts[n], cuts[n + 1])
+    for n in range(X):
+        part = slice(X - 1 - n, X - n)
         loads.append(
             pltpu.make_async_copy(pop_hbm.at[:, :, part], pop.at[:, :, part], load_sem.at[1 + n])
         )
@@ -237,39 +240,75 @@
         rows = slice(T * (t - 1), T * t)
         return jnp.where(lane < HALF, pop[1, OPPOSITE[i], x, rows], pop[1, i, x, rows])
 
+    beside = [blank, blank]
+
+    def put_beside(x, h, b, t, value):
+        n, at = (1, X - 1) if x == 0 else (0, 0)
+        j = (h * HALF + t * stride_t + (b * X + at) * 2) // 2
+        beside[n] = jnp.where(pair == j, roll(value, 2 * j + 1), beside[n])
+
     def pack_signs(x):
         for t in range(1, YT + 1):
+            rows = slice(T * (t - 1), T * t)
             for k in range(2):
                 value = S[k, 2 + x, T * t:T * t + T]
                 put(0, k, 0, t, x, value)
                 put(0, k, 1, t, x, value, inside=True)
-            for d in range(3):
-                put(*V_PLACE[d], t, x, V[d, 1 + x, T * (t - 1):T * t])
             if x in (0, X - 1):
+                for d in range(3):
+                    put_beside(x, *V_PLACE[d][1:], t, V[d, 1 + x, rows])
                 out_i, in_i = (Z_UP[1], Z_UP[2]) if x else (Z_UP[2], Z_UP[1])
-                rows = slice(T * (t - 1), T * t)
                 value = jnp.where(lane < HALF, pop[1, OPPOSITE[in_i], x, rows], pop[1, out_i, x, rows])
-                put(1, 1, 1, t, x, value)
-
-    loads[0].wait()
-    for n in range(2):
-        loads[1 + n].wait()
-        for x in range(cuts[n], cuts[n + 1]):
-            moments(x)
-        for x in range(cuts[n], cuts[n + 1]):
-            pack_signs(x)
-
+                put_beside(x, 1, 1, t, value)
+
+    top_z = me[2] == count[2] - 1
+    not_top = jnp.logical_not(top_z)
+
+    def tell(sem):
+        pl.semaphore_signal(sem, inc=1, device_id=partner, device_id_type=MESH)
+
+    def learn_far():
+        pl.semaphore_wait(barrier, far_count)
+        tell(far_sem)
+
+    corner = top_z & (me[0] == count[0] - 1)
     place = slot % X
 
     def edges(v, q):
         return jnp.where(upper, roll(v, (q - 1) * stride_t), roll(v, (q - YT) * stride_t))
 
-    for n in range(2):
-        if n == 0:
-            tile = jnp.where(place >= X - 2, packs[0], roll(packs[1], -2 * (X - 1)))
-        else:
-            tile = jnp.where(place < 2, packs[0], roll(packs[1], 2 * (X - 1)))
+    def make_diagonal(n):
+        tile = jnp.where((place >= X - 2) if n == 0 else (place < 2), packs[0], beside[n])
         XSND[n, 0] = jnp.where(tile_t == 0, edges(tile, 0), tile)
+
+    def send_diagonal(n):
+        side = 1 - 2 * n
+        for m, dz in enumerate((1, -1)):
+            send("zD", XSND.at[n, 0], ZD.at[m, n, 0], (side, 0, dz), 1)
+            for sy in y_sides:
+                send("zD", XSND.at[n, 0], ZD.at[m, n, 1 + y_slot[-sy]], (side, sy, dz), 1)
+
+    @pl.when(is_far & corner)
+    def _():
+        learn_far()
+
+    loads[0].wait()
+    for n in range(X):
+        loads[1 + n].wait()
+        moments(X - 1 - n)
+        pack_signs(X - 1 - n)
+        if n == 1:
+            make_diagonal(0)
+
+            @pl.when(is_near & corner)
+            def _():
+                pl.semaphore_wait(far_sem, 1)
+
+            @pl.when(corner)
+            def _():
+                send_diagonal(0)
+
+    make_diagonal(1)
 
     def ends(a, b):
         return jnp.where(upper, a, b)
@@ -286,16 +325,6 @@
             packed = jnp.where(at, roll_rows(fields[f], 2 * f), packed)
         XSND[n, 1] = packed
 
-    top_z = me[2] == count[2] - 1
-    not_top = jnp.logical_not(top_z)
-
-    def tell(sem):
-        pl.semaphore_signal(sem, inc=1, device_id=partner, device_id_type=MESH)
-
-    def learn_far():
-        pl.semaphore_wait(barrier, far_count)
-        tell(far_sem)
-
     first_up = lax.rem(me[0], 4) != 1
     sides = [jnp.where(first_up, 1, -1), jnp.where(first_up, -1, 1)]
 
@@ -315,18 +344,14 @@
             send("xB", pop.at[1, jnp.where(up, i, OPPOSITE[i]), jnp.where(up, X - 1, 0)],
                  XB.at[n, 3 + m], to, YT)
 
-    def send_diagonal():
-        for n, side in enumerate((1, -1)):
-            for m, dz in enumerate((1, -1)):
-                send("zD", XSND.at[n, 0], ZD.at[m, n, 0], (side, 0, dz), 1)
-                for sy in y_sides:
-                    send("zD", XSND.at[n, 0], ZD.at[m, n, 1 + y_slot[-sy]], (side, sy, dz), 1)
-
     ZS[5] = packs[0]
 
     def pack_faces():
+        packs[1] = jnp.where(place == X - 1, roll(beside[0], 2 * (X - 1)), roll(beside[1], -2 * (X - 1)))
         for x in range(X):
             for t in range(1, YT + 1):
+                for d in range(3) if 0 < x < X - 1 else ():
+                    put(*V_PLACE[d], t, x, V[d, 1 + x, T * (t - 1):T * t])
                 for g, i in enumerate(Z_UP):
                     put(*POP_PLACE[g], t, x, z_ends(i, x, t))
         merged = edges(packs[0], 0)
@@ -337,7 +362,7 @@
             ZS[m] = jnp.where(even, one, roll(two, 1))
             ZS[2 + m] = jnp.where(even, roll(two, -1), one)
         ZS[4] = merged
-        packs[2] = packs[3] = blank
+        packs[1] = packs[2] = packs[3] = blank
 
     def send_faces():
         for m, dz in enumerate((1, -1)):
@@ -345,23 +370,27 @@
             for sy in y_sides:
                 send("zF", ZS.at[4], ZF.at[m, 2 + y_slot[-sy]], (0, sy, dz), 1)
 
-    @pl.when(is_far & top_z)
+    late = top_z & jnp.logical_not(corner)
+
+    @pl.when(is_far & late)
     def _():
         learn_far()
 
-    @pl.when(is_near & top_z)
+    @pl.when(is_near & late)
     def _():
         pl.semaphore_wait(far_sem, 1)
 
-    counted = sent[0]
+    @pl.when(late)
+    def _():
+        send_diagonal(0)
 
     @pl.when(top_z)
     def _():
-        send_diagonal()
+        send_diagonal(1)
         pack_faces()
         send_faces()
 
-    sent[0] = counted
+    sent[0] = 0
 
     @pl.when(is_near)
     def _():
@@ -402,7 +431,8 @@
 
     @pl.when(not_top)
     def _():
-        send_diagonal()
+        send_diagonal(0)
+        send_diagonal(1)
         send_faces()
 
     send_x_bulk(sides[1])
@@ -688,6 +718,9 @@
     for x in range(1, X - 1):
         collide_own(x)
         collide_rows(x)
+    state = (pop, solid, post, zpost, signs, inside)
+    for x in range(1, X - 1):
+        stream(x, x - 1, state, reach(x, X))
 
     await_("zD", ZD)
     diags, far_signs = [], []
@@ -712,7 +745,7 @@
     for n in range(2):
         collide_corner(n)
     for x in range(1, X - 1):
-        stream(x, x - 1, (pop, solid, post, zpost, signs, inside))
+        stream(x, x - 1, state, [i for i in range(19) if i not in reach(x, X)])
     await_("xB", XB)
     for n in range(2):
         collide_plane(n)
@@ -768,7 +801,7 @@
             vmem(2, 2 + NY, T, LANES),
             vmem(2, 2, 1 + NY, T, LANES),
             vmem(tiles, T, LANES),
-            dma((3,)),
+            dma((X + 1,)),
             dma,
             dma((7,)),
             pltpu.SemaphoreType.REGULAR,

time: 12.4 us -> 12.2 us (0.984)
  Pallas kernels: 12.3 us -> 12 us
    pallas_call x1, Pallas kernels: 11.2 us -> 11 us  [body(): pl.pallas_call(step_kernel, out_shape=[pltpu.VMEM(a, b) for a, b in zip(s...]
where the time goes in v7:
time: 12.2 us; the launch traced here: 12 us
  Pallas kernels  12 us (98%)
    pallas_call x1, Pallas kernels, body(): pl.pallas_call(step_kernel, out_shape=[pltpu.VMEM(a, b) for a, b in zip(s...  11 us
    pallas_call x1, Pallas kernels, body(): pl.pallas_call(finish_kernel, out_shape=jax.ShapeDtypeStruct(populations....  1.07 us

profile of v7, /device:TPU:0, one launch (start us, length us, event | category | flops | bytes accessed | tf_op | source)
XLA Modules:
  0.0 12.0 jit_solution(19494214277087988)
XLA Ops:
  0.0 11.0 %shard_map.28 = (f32[2,19,4,16,128]{4,3,2,1,0:T(8,128)S(1)}, s32[4,16,128]{2,1,0:T(8,128)S(1)}, f32[2,19,6,32,128]{4,3,2,1,0:T(8,128)S(1)}, f32[2,5,4,16,128]{4,...) custom-call(f32[2,19,4,16,128]{4,3,2,1,0:T(8,128)} %pop_hbm.1, ...), custom_call_target="tpu_custom_call" | custom-call | tf_op jit(solution)/shard_map/pallas_call | solution.py:779
  11.0 1.1 %shard_map.29 = f32[2,19,4,16,128]{4,3,2,1,0:T(8,128)} custom-call(f32[2,19,4,16,128]{4,3,2,1,0:T(8,128)S(1)} %get-tuple-element.11.pop, s32[4,16,128]{2,1,0:T(8,128)S(1)} %get-tuple-element.12.solid, f32[2,19,6,32,128]{4,3,2,1,0:T(8,128)S(1)} %get-tuple-element.13.post, f32[2,5,4,16,128]{4,3,2,1,0:T(8,128)S(1)} %get-tuple-element.14.zpost, ...), custom_call_target="tpu_custom_call" | custom-call | tf_op jit(solution)/shard_map/pallas_call | solution.py:814

commit v8 on v7

--- a/solution.py
+++ b/solution.py
@@ -184,16 +184,16 @@
     GROUPS = {"y": 0, "yX": 1, "xS": 2, "xE": 3, "zF": 4, "zD": 5, "xB": 6}
     sent = [0]
 
-    def send(group, src, dst, offset, tiles):
+    def send(group, src, dst, offset, tiles, first=False):
         pltpu.make_async_remote_copy(
             src_ref=src,
             dst_ref=dst,
-            send_sem=send_sem,
+            send_sem=send_sem.at[1 if first else 0],
             recv_sem=recv_sem.at[GROUPS[group]],
             device_id=device(offset),
             device_id_type=MESH,
         ).start()
-        sent[0] += tiles
+        sent[0] += 0 if first else tiles
 
     def await_(group, ref):
         pltpu.make_async_copy(ref, ref, recv_sem.at[GROUPS[group]]).wait()
@@ -335,14 +335,14 @@
         send("xS", S.at[:, pl.ds(src, 2), inner], S.at[:, pl.ds(dst, 2), inner],
              (side, 0, 0), 4 * YT)
 
-    def send_x_bulk(side):
+    def send_x_bulk(side, first):
         up = side > 0
         n = jnp.where(up, 0, 1)
         to = (side, 0, 0)
-        send("xB", V.at[:, jnp.where(up, X, 1), 0:Y], XB.at[n, 0:3], to, 3 * YT)
+        send("xB", V.at[:, jnp.where(up, X, 1), 0:Y], XB.at[n, 0:3], to, 3 * YT, first)
         for m, i in enumerate(X_UP):
             send("xB", pop.at[1, jnp.where(up, i, OPPOSITE[i]), jnp.where(up, X - 1, 0)],
-                 XB.at[n, 3 + m], to, YT)
+                 XB.at[n, 3 + m], to, YT, first)
 
     ZS[5] = packs[0]
 
@@ -372,6 +372,10 @@
 
     late = top_z & jnp.logical_not(corner)
 
+    @pl.when(late)
+    def _():
+        pack_faces()
+
     @pl.when(is_far & late)
     def _():
         learn_far()
@@ -382,9 +386,11 @@
 
     @pl.when(late)
     def _():
+        send_faces()
         send_diagonal(0)
-
-    @pl.when(top_z)
+        send_diagonal(1)
+
+    @pl.when(corner)
     def _():
         send_diagonal(1)
         pack_faces()
@@ -415,7 +421,7 @@
         for m, i in enumerate(Y_UP):
             i = i if side > 0 else OPPOSITE[i]
             send("y", pop.at[1, i, :, tile], YR.at[n, 5 + m], to, X)
-    send_x_bulk(sides[0])
+    send_x_bulk(sides[0], True)
 
     @pl.when(not_top)
     def _():
@@ -435,7 +441,8 @@
         send_diagonal(1)
         send_faces()
 
-    send_x_bulk(sides[1])
+    pltpu.make_async_copy(XB.at[0], XB.at[0], send_sem.at[1]).wait()
+    send_x_bulk(sides[1], False)
     await_("y", YR)
     for x in range(X):
         for k in range(2):
@@ -585,12 +592,6 @@
             post[k, up, 1 + x, low] = value
             post[k, down, 1 + x, high] = value
 
-    def x_up(v):
-        return roll(v, -2)
-
-    def x_down(v):
-        return roll(v, 2)
-
     def y_up(v, n=0):
         r = roll_rows(v, -1)
         return jnp.where(row == T - 1, roll(r, n - stride_t), roll(r, n))
@@ -607,18 +608,16 @@
             jnp.where(lower, other1, t1),
         ]
         p0, p1, p2 = jnp.abs(s0), jnp.abs(s1), jnp.abs(s2)
-        xs = [x_up(v) + x_down(v) for v in (p0, p1, p2)]
-        ys = [y_up(v) + y_down(v) for v in (p0, p1, p2)]
         g = 2.0 * p1 + (p0 + p2)
-        a = g + ys[1]
-        b = g + xs[1]
-        c0 = 2.0 * p0 + (xs[0] + ys[0])
-        c2 = 2.0 * p2 + (xs[2] + ys[2])
         sign = jnp.where(even, 1.0, -1.0)
+        d = (p0 - p2) * sign
+        up_up, up_down = y_up(p1, HALF - 2), y_down(p1, HALF - 2)
+        down_up, down_down = y_up(p1, HALF + 2), y_down(p1, HALF + 2)
         grads = [
-            roll(a, HALF - 2) - roll(a, HALF + 2),
-            y_up(b, HALF) - y_down(b, HALF),
-            roll((c0 - c2) * sign, HALF),
+            (roll(g, HALF - 2) - roll(g, HALF + 2)) + ((up_up + up_down) - (down_up + down_down)),
+            (y_up(g, HALF) - y_down(g, HALF)) + ((up_up + down_up) - (up_down + down_down)),
+            (2.0 * roll(d, HALF) + (roll(d, HALF - 2) + roll(d, HALF + 2)))
+            + (y_up(d, HALF) + y_down(d, HALF)),
         ]
         factor = jnp.where(lower, COUPLING * RELAX[0] / 36.0, COUPLING * RELAX[1] / 36.0)
         u = [common[d] - factor * grads[d] for d in range(3)]
@@ -676,13 +675,6 @@
         return low_part if NY == 1 else ends(low_part, high_part)
 
     top = stride_t * (YT + 1)
-
-    def assemble(middle, left, right, shift_left, shift_right):
-        return jnp.where(
-            slot < 2,
-            roll(left, 2 * shift_left),
-            jnp.where(slot >= X + 2, roll(right, 2 * shift_right), middle),
-        )
 
     s0 = roll(ZS[5], 4)
     for p in range(XX):
@@ -723,25 +715,34 @@
         stream(x, x - 1, state, reach(x, X))
 
     await_("zD", ZD)
-    diags, far_signs = [], []
+    bases, row_parts, far_signs = [], [], []
     for n in range(2):
         merged = [jnp.where(even, ZD[0, n, q], ZD[1, n, q]) for q in range(1 + NY)]
         w = by_row(merged[1 + y_slot[1]], merged[1 + y_slot[-1]])
-        far_signs.append(swap(jnp.where(tile_t == 0, w, merged[0])))
-        diags.append(with_rows(merged[0], w, roll(w, top)))
+        bases.append(jnp.where(tile_t == 0, w, merged[0]))
+        row_parts.append(w)
+        far_signs.append(swap(bases[n]))
+
+    def moved(n, shift):
+        return jnp.where(
+            tile_t == YT + 1, roll(row_parts[n], 2 * shift + top), roll(bases[n], 2 * shift)
+        )
+
+    def assemble(middle, shift_left, shift_right):
+        outside = jnp.where(slot < 2, moved(0, shift_left), moved(1, shift_right))
+        return jnp.where((slot < 2) | (slot >= X + 2), outside, middle)
+
+    s1, s2 = [assemble(center[0][b], -(b * X + X - 2), X + 2 - b * X) for b in range(2)]
+    t1, t2 = [assemble(center[1][b], 1 - b * X, 3 - b * X) for b in range(2)]
     for m in range(2):
         complete(m, far_signs[0], X - 2 + m)
         complete(X + 2 + m, far_signs[1], m)
-    s1, s2 = [
-        assemble(center[0][b], *diags, -(b * X + X - 2), X + 2 - b * X) for b in range(2)
-    ]
-    t1, t2 = [assemble(center[1][b], *diags, 1 - b * X, 3 - b * X) for b in range(2)]
     for p in outer:
         sums(p)
+    collide_z(s0, s1, s2, t1, t2, olds)
     for x in (0, X - 1):
         collide_own(x)
         collide_rows(x)
-    collide_z(s0, s1, s2, t1, t2, olds)
     for n in range(2):
         collide_corner(n)
     for x in range(1, X - 1):
@@ -750,7 +751,7 @@
     for n in range(2):
         collide_plane(n)
     assert sent[0] == tally.shape[0]
-    pltpu.make_async_copy(tally, tally, send_sem).wait()
+    pltpu.make_async_copy(tally, tally, send_sem.at[0]).wait()
 
 
 def body(populations, solid):
@@ -761,7 +762,7 @@
     XX = X + 4
     NY = 1 if lax.axis_size("gy") == 2 else 2
     YT = Y // T
-    tiles = 20 * X + 24 * YT + 24 + 8 * NY
+    tiles = 20 * X + 16 * YT + 24 + 8 * NY
 
     def vmem(*shape):
         return pltpu.VMEM(shape, f32)
@@ -802,7 +803,7 @@
             vmem(2, 2, 1 + NY, T, LANES),
             vmem(tiles, T, LANES),
             dma((X + 1,)),
-            dma,
+            dma((2,)),
             dma((7,)),
             pltpu.SemaphoreType.REGULAR,
             pltpu.SemaphoreType.REGULAR,

time: 12.2 us -> 12.1 us (level)
  Pallas kernels: 12 us -> 11.8 us
    pallas_call x1, Pallas kernels: 11 us -> 10.8 us  [body(): pl.pallas_call(step_kernel, out_shape=[pltpu.VMEM(a, b) for a, b in zip(s...]
where the time goes in v8:
time: 12.1 us; the launch traced here: 11.8 us
  Pallas kernels  11.8 us (98%)
    pallas_call x1, Pallas kernels, body(): pl.pallas_call(step_kernel, out_shape=[pltpu.VMEM(a, b) for a, b in zip(s...  10.8 us
    pallas_call x1, Pallas kernels, body(): pl.pallas_call(finish_kernel, out_shape=jax.ShapeDtypeStruct(populations....  1.07 us

profile of v8, /device:TPU:0, one launch (start us, length us, event | category | flops | bytes accessed | tf_op | source)
XLA Modules:
  0.0 11.8 jit_solution(12183573134430891168)
XLA Ops:
  0.0 10.8 %shard_map.28 = (f32[2,19,4,16,128]{4,3,2,1,0:T(8,128)S(1)}, s32[4,16,128]{2,1,0:T(8,128)S(1)}, f32[2,19,6,32,128]{4,3,2,1,0:T(8,128)S(1)}, f32[2,5,4,16,128]{4,...) custom-call(f32[2,19,4,16,128]{4,3,2,1,0:T(8,128)} %pop_hbm.1, ...), custom_call_target="tpu_custom_call" | custom-call | tf_op jit(solution)/shard_map/pallas_call | solution.py:780
  10.8 1.1 %shard_map.29 = f32[2,19,4,16,128]{4,3,2,1,0:T(8,128)} custom-call(f32[2,19,4,16,128]{4,3,2,1,0:T(8,128)S(1)} %get-tuple-element.11.pop, s32[4,16,128]{2,1,0:T(8,128)S(1)} %get-tuple-element.12.solid, f32[2,19,6,32,128]{4,3,2,1,0:T(8,128)S(1)} %get-tuple-element.13.post, f32[2,5,4,16,128]{4,3,2,1,0:T(8,128)S(1)} %get-tuple-element.14.zpost, ...), custom_call_target="tpu_custom_call" | custom-call | tf_op jit(solution)/shard_map/pallas_call | solution.py:815

commit v9 on v8

--- a/solution.py
+++ b/solution.py
@@ -99,7 +99,7 @@
 
 def step_kernel(pop_hbm, solid_hbm, pop, solid, post, zpost, signs, inside, S, SU, SD, psi, H, O, A, V,
                 YR, WP, XB, XWP, XSND, XE, ZS, YX, ZF, ZD, tally, load_sem, send_sem, recv_sem,
-                near_sem, far_sem):
+                told_sem):
     X, Y, Z = solid.shape
     YT = Y // T
     inner = slice(T, T + Y)
@@ -269,7 +269,7 @@
 
     def learn_far():
         pl.semaphore_wait(barrier, far_count)
-        tell(far_sem)
+        tell(told_sem)
 
     corner = top_z & (me[0] == count[0] - 1)
     place = slot % X
@@ -302,7 +302,7 @@
 
             @pl.when(is_near & corner)
             def _():
-                pl.semaphore_wait(far_sem, 1)
+                pl.semaphore_wait(told_sem, 1)
 
             @pl.when(corner)
             def _():
@@ -382,7 +382,7 @@
 
     @pl.when(is_near & late)
     def _():
-        pl.semaphore_wait(far_sem, 1)
+        pl.semaphore_wait(told_sem, 1)
 
     @pl.when(late)
     def _():
@@ -401,11 +401,11 @@
     @pl.when(is_near)
     def _():
         pl.semaphore_wait(barrier, near_count)
-        tell(near_sem)
+        tell(told_sem)
 
     @pl.when(is_far)
     def _():
-        pl.semaphore_wait(near_sem, 1)
+        pl.semaphore_wait(told_sem, 1)
 
     send_x_signs(sides[0])
     send_x_signs(sides[1])
@@ -433,7 +433,7 @@
 
     @pl.when(is_near & not_top)
     def _():
-        pl.semaphore_wait(far_sem, 1)
+        pl.semaphore_wait(told_sem, 1)
 
     @pl.when(not_top)
     def _():
@@ -441,8 +441,6 @@
         send_diagonal(1)
         send_faces()
 
-    pltpu.make_async_copy(XB.at[0], XB.at[0], send_sem.at[1]).wait()
-    send_x_bulk(sides[1], False)
     await_("y", YR)
     for x in range(X):
         for k in range(2):
@@ -643,6 +641,8 @@
     for x in range(X):
         prepare(2 + x)
 
+    pltpu.make_async_copy(XB.at[0], XB.at[0], send_sem.at[1]).wait()
+    send_x_bulk(sides[1], False)
     await_("xS", S.at[:, 0:4, inner])
     for n, side in enumerate((1, -1)):
         wide = slice(Y, Y + T) if side > 0 else slice(T, 2 * T)
@@ -806,7 +806,6 @@
             dma((2,)),
             dma((7,)),
             pltpu.SemaphoreType.REGULAR,
-            pltpu.SemaphoreType.REGULAR,
         ],
         compiler_params=pltpu.CompilerParams(
             collective_id=0, has_side_effects=True, vmem_limit_bytes=24 * 2**20

time: 12.1 us -> 12 us (level)
  no operation moved by 1% of the time
where the time goes in v9:
time: 12 us; the launch traced here: 11.8 us
  Pallas kernels  11.8 us (98%)
    pallas_call x1, Pallas kernels, body(): pl.pallas_call(step_kernel, out_shape=[pltpu.VMEM(a, b) for a, b in zip(s...  10.8 us
    pallas_call x1, Pallas kernels, body(): pl.pallas_call(finish_kernel, out_shape=jax.ShapeDtypeStruct(populations....  1.07 us

profile of v9, /device:TPU:0, one launch (start us, length us, event | category | flops | bytes accessed | tf_op | source)
XLA Modules:
  0.0 11.8 jit_solution(11513451777946761553)
XLA Ops:
  0.0 10.8 %shard_map.28 = (f32[2,19,4,16,128]{4,3,2,1,0:T(8,128)S(1)}, s32[4,16,128]{2,1,0:T(8,128)S(1)}, f32[2,19,6,32,128]{4,3,2,1,0:T(8,128)S(1)}, f32[2,5,4,16,128]{4,...) custom-call(f32[2,19,4,16,128]{4,3,2,1,0:T(8,128)} %pop_hbm.1, ...), custom_call_target="tpu_custom_call" | custom-call | tf_op jit(solution)/shard_map/pallas_call | solution.py:780
  10.8 1.1 %shard_map.29 = f32[2,19,4,16,128]{4,3,2,1,0:T(8,128)} custom-call(f32[2,19,4,16,128]{4,3,2,1,0:T(8,128)S(1)} %get-tuple-element.11.pop, s32[4,16,128]{2,1,0:T(8,128)S(1)} %get-tuple-element.12.solid, f32[2,19,6,32,128]{4,3,2,1,0:T(8,128)S(1)} %get-tuple-element.13.post, f32[2,5,4,16,128]{4,3,2,1,0:T(8,128)S(1)} %get-tuple-element.14.zpost, ...), custom_call_target="tpu_custom_call" | custom-call | tf_op jit(solution)/shard_map/pallas_call | solution.py:814
